TPU v7x, 256 devices: a whole 4x4x8 slice. The times are simulated.
256 devices in a mesh: frame: 32 (over x, z_hi, core), coil: 8 (over z_lo, y).
Axes of the slice: x: 4, y: 4, z: 8 (z_hi: 4, z_lo: 2; z = z_hi * 2 + z_lo), core: 2. Of those that a mesh axis runs over, the one named last changes fastest.
Arguments:
- kspace: bfloat16 [32, 64, 256, 512], P('frame', 'coil'), may hold values from -6 to 6
- sens: bfloat16 [64, 256, 512], P('coil'), may hold values from -0.5 to 0.5
- mask: int32 [32, 64, 256], P('frame', 'coil'), may hold values 0 or 1
- image: float32 [32, 256, 512], P('frame', 'coil'), may hold values from -6 to 6
- w_first: bfloat16 [3, 3, 3, 64, 2], replicated, may hold values from -0.875 to 0.875
- b_first: float32 [64], replicated, may hold values from -3 to 3
- w_mid: bfloat16 [3, 3, 3, 64, 64], replicated, may hold values from -0.15625 to 0.15625
- b_mid: float32 [64], replicated, may hold values from -3 to 3
- w_last: bfloat16 [3, 3, 3, 2, 64], replicated, may hold values from -0.15625 to 0.15625
Outputs:
- recon: float32 [32, 256, 512], P('frame', 'coil')
Inputs may be any that keep to these rules, and one draw needn't show every extreme that they name: mask is 1 on the acquired phase-encoding lines of a frame and coil and 0 on the others.
All inputs are finite; a program needn't handle non-finite values. No bound on the sum of `mask` on one device may be relied on, other than what follows from the above.
Results may differ from a plain program's by a relative error of at most 0.006.
Values may be sent and summed in bfloat16 or wider, within the bound.
A program may use at most 64 MiB of HBM per device.

v0:
```python
import math

import jax
import jax.numpy as jnp
from jax import lax
from jax.sharding import PartitionSpec as P

step_size = 1.0


def from_everyone(shard, axis):
    devices = lax.axis_size(axis)
    return lax.all_to_all(
        jnp.broadcast_to(shard[None], (devices, *shard.shape)), axis, 0, 0, tiled=True
    )


def laid_out(parts, dim):
    shape = list(parts.shape[1:])
    shape[dim] *= parts.shape[0]
    return jnp.moveaxis(parts, 0, dim).reshape(shape)


def collect(shard, axis, dim):
    parts = from_everyone(shard, axis)
    return laid_out(parts, dim)


def cut_along(shard, dim, devices):
    shape = shard.shape
    parts = shard.reshape(*shape[:dim], devices, shape[dim] // devices, *shape[dim + 1 :])
    return jnp.moveaxis(parts, dim, 0)


def sent_and_summed(shard, axis, dim):
    parts = cut_along(shard, dim, lax.axis_size(axis))
    arrived = lax.all_to_all(parts, axis, split_axis=0, concat_axis=0, tiled=True)
    return arrived.sum(axis=0)


def with_halo(shard, sides, width):
    for axis, dim in sides:
        devices, length = (lax.axis_size(axis), shard.shape[dim])
        up = [(i, (i + 1) % devices) for i in range(devices - 1)]
        down = [(j, i) for i, j in up]
        last = lax.slice_in_dim(shard, length - width, length, axis=dim)
        leading = lax.slice_in_dim(shard, 0, width, axis=dim)
        before = lax.ppermute(last, axis, up)
        after = lax.ppermute(leading, axis, down)
        shard = jnp.concatenate([before, shard, after], axis=dim)
    return shard


def dft_parts(order):
    indices = jnp.arange(order, dtype=jnp.int32)
    phases = indices[:, None] * indices[None, :] % order
    angles = phases.astype(jnp.float32) * (2.0 * math.pi / order)
    factor = 1.0 / math.sqrt(order)
    return (
        (jnp.cos(angles) * factor).astype(jnp.bfloat16),
        (-jnp.sin(angles) * factor).astype(jnp.bfloat16),
    )


def column_tables(real_part, imag_part):
    ahead = jnp.concatenate(
        [jnp.concatenate([real_part, imag_part], 1), jnp.concatenate([-imag_part, real_part], 1)], 0
    )
    behind = jnp.concatenate(
        [jnp.concatenate([real_part, -imag_part], 1), jnp.concatenate([imag_part, real_part], 1)], 0
    )
    return (ahead, behind)


def swapped(values):
    half_width = values.shape[-1] // 2
    return jnp.concatenate([-values[..., half_width:], values[..., :half_width]], -1)


def complex_mul(first, second):
    half_width = first.shape[-1] // 2
    first_re, first_im = (first[..., :half_width], first[..., half_width:])
    second_re, second_im = (second[..., :half_width], second[..., half_width:])
    return jnp.concatenate(
        [first_re * second_re - first_im * second_im, first_re * second_im + first_im * second_re],
        -1,
    )


def conj_mul(first, second):
    half_width = first.shape[-1] // 2
    first_re, first_im = (first[..., :half_width], first[..., half_width:])
    second_re, second_im = (second[..., :half_width], second[..., half_width:])
    return jnp.concatenate(
        [first_re * second_re + first_im * second_im, first_re * second_im - first_im * second_re],
        -1,
    )


def data_step(image_now, kspace, sens, mask, row_real, row_imag, ahead, behind):
    f32 = jnp.float32
    sens_rows = sens.astype(f32)
    coil_image = complex_mul(
        sens_rows[None], collect(image_now.astype(jnp.bfloat16), "coil", 1).astype(f32)[:, None]
    ).astype(jnp.bfloat16)
    cols_spectrum = jnp.einsum(
        "fcrm,mn->fcrn", coil_image, ahead, preferred_element_type=f32
    ).astype(jnp.bfloat16)
    stacked = jnp.concatenate([cols_spectrum, swapped(cols_spectrum)], 2)
    row_ahead = jnp.concatenate([row_real, row_imag], 1)
    estimate = jnp.einsum("kr,fcrn->fckn", row_ahead, stacked, preferred_element_type=f32)
    misfit = (mask.astype(f32)[..., None] * (estimate - kspace.astype(f32))).astype(jnp.bfloat16)
    back_cols = jnp.einsum("fckm,mn->fckn", misfit, behind, preferred_element_type=f32).astype(
        jnp.bfloat16
    )
    stacked_back = jnp.concatenate([back_cols, swapped(back_cols)], 2)
    lower = -row_imag
    row_behind = jnp.concatenate([row_real, lower], 1)
    back_image = jnp.einsum("rk,fckn->fcrn", row_behind, stacked_back, preferred_element_type=f32)
    sens_rows = sens.astype(f32)
    term = jnp.sum(conj_mul(sens_rows[None], back_image), 1)
    summed = sent_and_summed(jnp.moveaxis(term, 1, 0), "coil", 0)
    return image_now - step_size * jnp.moveaxis(summed, 0, 1)


def with_rims(hidden):
    wider = with_halo(hidden, (("frame", 0),), 1)
    return with_halo(wider, (("coil", 1),), 1)


def conv_layer(padded, weight):
    frames = padded.shape[0] - 2
    rows = padded.shape[1] - 2
    out_chan = weight.shape[3]
    in_chan = weight.shape[4]
    window = jnp.concatenate(
        [
            padded[tap_frame : tap_frame + frames, tap_row : tap_row + rows]
            for tap_frame in range(3)
            for tap_row in range(3)
        ],
        2,
    )
    matrix = jnp.transpose(weight, (2, 3, 0, 1, 4)).reshape(3 * out_chan, 9 * in_chan)
    taps_out = jnp.einsum("km,frmn->frkn", matrix, window, preferred_element_type=jnp.float32)
    left_taps = taps_out[:, :, :out_chan]
    centre = taps_out[:, :, out_chan : 2 * out_chan]
    right_taps = taps_out[:, :, 2 * out_chan :]
    zeros_col = jnp.zeros_like(left_taps[..., :1])
    return (
        centre
        + jnp.concatenate([zeros_col, left_taps[..., :-1]], -1)
        + jnp.concatenate([right_taps[..., 1:], zeros_col], -1)
    )


def denoise(image_now, w_first, b_first, w_mid, b_mid, w_last):
    frames, rows, double = image_now.shape
    hidden = image_now.reshape(frames, rows, 2, double // 2).astype(jnp.bfloat16)
    first = jax.nn.relu(
        conv_layer(with_rims(hidden), w_first) + b_first[None, None, :, None]
    ).astype(jnp.bfloat16)
    second = jax.nn.relu(conv_layer(with_rims(first), w_mid) + b_mid[None, None, :, None]).astype(
        jnp.bfloat16
    )
    update = conv_layer(with_rims(second), w_last)
    return image_now + update.reshape(frames, rows, double)


def shards(kspace, sens, mask, image, w_first, b_first, w_mid, b_mid, w_last):
    row_real, row_imag = dft_parts(sens.shape[1])
    col_real, col_imag = dft_parts(sens.shape[2] // 2)
    ahead, behind = column_tables(col_real, col_imag)
    image_now = image
    image_now = data_step(image_now, kspace, sens, mask, row_real, row_imag, ahead, behind)
    image_now = denoise(image_now, w_first, b_first, w_mid, b_mid, w_last)
    return image_now


def solution(mesh):
    in_specs = (
        P("frame", "coil", None, None),
        P("coil", None, None),
        P("frame", "coil", None),
        P("frame", "coil", None),
        P(),
        P(),
        P(),
        P(),
        P(),
    )
    out_specs = P("frame", "coil", None)
    return jax.shard_map(shards, mesh=mesh, in_specs=in_specs, out_specs=out_specs, check_vma=False)
```

profile of v0, /device:TPU:30, one launch (start us, length us, event | category | flops | bytes accessed | tf_op | source)
XLA Modules:
  0.0 167.6 jit_solution(2996725235543317200)
XLA Ops:
  0.0 0.8 convert_bitcast_fusion.2
  0.8 0.7 broadcast_in_dim.12
  1.6 6.0 %all-to-all-start = ((bf16[8,1,32,512]{3,2,1,0:T(8,128)(2,1)}), bf16[8,1,32,512]{3,2,1,0:T(8,128)(2,1)S(1)}, u32[]{:S(2)}, u32[]{:S(2)}) async-start(bf16[8,1,32,512]{3,2,1,0:T(8,128)(2,1)} %broadcast_in_dim.12), calls=%async_computation | async-start | bytes 524288 | tf_op jit(solution)/shard_map/all_to_all | solution.py:13
  7.6 1.1 multiply_convert_fusion
  8.8 4.1 %copy.24 = bf16[1,8,256,512]{2,3,1,0:T(8,128)(2,1)} copy(bf16[1,8,256,512]{3,2,1,0:T(8,128)(2,1)} %param.9) | data formatting | bytes 4194304 | tf_op args[0]
  12.8 1.0 fusion.73
  13.8 2.5 %bitcast_convert_fusion = f32[1,8,256,512]{3,2,1,0:T(8,128)} fusion(bf16[8,256,512]{2,1,0:T(8,128)(2,1)S(1)} %copy-done.1), kind=kLoop, calls=%fused_computation.39 | loop fusion | flops 1048576 | bytes 6291456 | tf_op jit(solution)/shard_map/broadcast_in_dim | solution.py:121
  16.5 2.8 %fusion.41 = (bf16[8,256,256]{2,1,0:T(8,128)(2,1)S(1)}, bf16[8,256,256]{2,1,0:T(8,128)(2,1)S(1)}) fusion(f32[1,8,256,512]{3,2,1,0:T(8,128)} %bitcast_convert_fusion, f32[256,256]{1,0:T(8,128)S(1)} %get-tuple-element.22, f32[256,256]{1,0:T(8,128)S(1)} %get-tuple-element.21), kind=kLoop, calls=%fused_computation.47 | loop fusion | flops 4194304 | bytes 6815744 | tf_op jit(solution)/shard_map/concatenate | solution.py:84
  19.3 1.3 convert_bitcast_fusion.1
  20.6 1.2 slice_negate_fusion.1
  22.3 1.0 copy-done.2
  23.3 7.7 %convert_bitcast_fusion = bf16[1,8,256,512]{3,2,1,0:T(8,128)(2,1)} fusion(bf16[1,8,256,512]{2,3,1,0:T(8,128)(2,1)S(1)} %copy-done.2, bf16[1,8,256,256]{3,2,1,0:T(8,128)(2,1)} %get-tuple-element.20, bf16[1,8,256,256]{3,2,1,0:T(8,128)(2,1)S(1)} %get-tuple-element.19, bf16[1,8,256,512]{3,2,1,0:T(8,128)(2,1)} %copy-done.4, ...), kind=kOutput, calls=%fused_computation.42 | convolution fusion | flops 2167930880 | bytes 8790016 | tf_op jit(solution)/shard_map/fckm,mn->fckn/dot_general | solution.py:113
  31.0 1.8 %slice_negate_fusion = (bf16[1,8,256,256]{3,2,1,0:T(8,128)(2,1)S(1)}, bf16[1,8,256,256]{3,2,1,0:T(8,128)(2,1)S(1)}) fusion(bf16[1,8,256,512]{3,2,1,0:T(8,128)(2,1)} %convert_bitcast_fusion), kind=kLoop, calls=%fused_computation.73 | loop fusion | flops 524288 | bytes 4194304 | tf_op jit(solution)/shard_map/neg | solution.py:77
  33.2 1.2 fusion.19
  34.5 0.9 copy-done
  35.4 0.6 multiply_add_fusion
  36.4 12.5 %all_to_all.10 = f32[8,32,1,512]{3,1,2,0:T(8,128)S(1)} all-to-all(f32[8,32,1,512]{3,1,2,0:T(8,128)S(1)} %bitcast.109), channel_id=1, replica_groups=mesh['frame'=32,'coil'=8] {'coil'}, dimensions={0} | all-to-all | bytes 1048576 | tf_op jit(solution)/shard_map/all_to_all | solution.py:37
  49.0 1.9 %collective-permute-start = (bf16[1,32,2,256]{3,2,1,0:T(2,128)(2,1)S(1)}, bf16[1,32,2,256]{3,2,1,0:T(2,128)(2,1)S(1)}, u32[]{:S(2)}, u32[]{:S(2)}) collective-permute-start(bf16[1,32,2,256]{3,2,1,0:T(2,128)(2,1)S(1)} %convert_element_type.117), channel_id=1, source_target_pairs={{0,8},{8,16},{16,24},{24,32},{32,40},{40,48},{48,56},{56,64},{64,7... | collective-permute-start | bytes 98312 | tf_op jit(solution)/shard_map/ppermute | solution.py:48
  50.9 6.7 %collective-permute-start.1 = (bf16[1,32,2,256]{3,2,1,0:T(2,128)(2,1)S(1)}, bf16[1,32,2,256]{3,2,1,0:T(2,128)(2,1)S(1)}, u32[]{:S(2)}, u32[]{:S(2)}) collective-permute-start(bf16[1,32,2,256]{3,2,1,0:T(2,128)(2,1)S(1)} %convert_element_type.117), channel_id=1, source_target_pairs={{8,0},{16,8},{24,16},{32,24},{40,32},{48,40},{56,48},{64,56},{72,6... | collective-permute-start | bytes 98312 | tf_op jit(solution)/shard_map/ppermute | solution.py:49
  57.7 1.5 collective-permute-done.1
  59.2 4.4 %collective-permute-start.2 = (bf16[3,1,2,256]{3,2,1,0:T(2,128)(2,1)S(1)}, bf16[3,1,2,256]{3,2,1,0:T(2,128)(2,1)S(1)}, u32[]{:S(2)}, u32[]{:S(2)}) collective-permute-start(bf16[3,1,2,256]{3,2,1,0:T(2,128)(2,1)S(1)} %get-tuple-element.35), channel_id=1, source_target_pairs={{0,1},{1,2},{2,3},{3,4},{4,5},{5,6},{6,7},{8,9},{9,10},{10,11},{11... | collective-permute-start | bytes 9224 | tf_op jit(solution)/shard_map/ppermute | solution.py:48
  63.6 2.1 %collective-permute-start.3 = (bf16[3,1,2,256]{3,2,1,0:T(2,128)(2,1)S(1)}, bf16[3,1,2,256]{3,2,1,0:T(2,128)(2,1)S(1)}, u32[]{:S(2)}, u32[]{:S(2)}) collective-permute-start(bf16[3,1,2,256]{3,2,1,0:T(2,128)(2,1)S(1)} %get-tuple-element.34), channel_id=1, source_target_pairs={{1,0},{2,1},{3,2},{4,3},{5,4},{6,5},{7,6},{9,8},{10,9},{11,10},{12... | collective-permute-start | bytes 9224 | tf_op jit(solution)/shard_map/ppermute | solution.py:49
  65.8 5.4 %collective-permute-done.3 = bf16[3,1,2,256]{3,2,1,0:T(2,128)(2,1)S(1)} collective-permute-done((bf16[3,1,2,256]{3,2,1,0:T(2,128)(2,1)S(1)}, bf16[3,1,2,256]{3,2,1,0:T(2,128)(2,1)S(1)}, u32[]{:S(2)}, u32[]{:S(2)}) %collective-permute-start.3) | collective-permute-done | bytes 3104 | tf_op jit(solution)/shard_map/ppermute | solution.py:49
  71.8 1.0 convolution_bitcast_fusion
  72.8 0.7 fusion.81
  73.6 0.8 fusion.27
  74.4 2.2 %collective-permute-start.4 = (bf16[1,32,64,256]{3,2,1,0:T(8,128)(2,1)S(1)}, bf16[1,32,64,256]{3,2,1,0:T(8,128)(2,1)S(1)}, u32[]{:S(2)}, u32[]{:S(2)}) collective-permute-start(bf16[1,32,64,256]{3,2,1,0:T(8,128)(2,1)S(1)} %fusion.27), channel_id=1, source_target_pairs={{0,8},{8,16},{16,24},{24,32},{32,40},{40,48},{48,56},{56,64},{64,7... | collective-permute-start | bytes 3145736 | tf_op jit(solution)/shard_map/ppermute | solution.py:48
  76.6 6.5 %collective-permute-start.5 = (bf16[1,32,64,256]{3,2,1,0:T(8,128)(2,1)S(1)}, bf16[1,32,64,256]{3,2,1,0:T(8,128)(2,1)S(1)}, u32[]{:S(2)}, u32[]{:S(2)}) collective-permute-start(bf16[1,32,64,256]{3,2,1,0:T(8,128)(2,1)S(1)} %fusion.27), channel_id=1, source_target_pairs={{8,0},{16,8},{24,16},{32,24},{40,32},{48,40},{56,48},{64,56},{72,6... | collective-permute-start | bytes 3145736 | tf_op jit(solution)/shard_map/ppermute | solution.py:49
  83.1 17.6 %collective-permute-done.4 = bf16[1,32,64,256]{3,2,1,0:T(8,128)(2,1)S(1)} collective-permute-done((bf16[1,32,64,256]{3,2,1,0:T(8,128)(2,1)S(1)}, bf16[1,32,64,256]{3,2,1,0:T(8,128)(2,1)S(1)}, u32[]{:S(2)}, u32[]{:S(2)}) %collective-permute-start.4) | collective-permute-done | bytes 1048608 | tf_op jit(solution)/shard_map/ppermute | solution.py:48
  100.7 1.5 collective-permute-done.5
  102.3 0.7 pad_maximum_fusion.23
  103.0 3.9 %collective-permute-start.6 = (bf16[3,1,64,256]{3,2,1,0:T(8,128)(2,1)}, bf16[3,1,64,256]{3,2,1,0:T(8,128)(2,1)S(1)}, u32[]{:S(2)}, u32[]{:S(2)}) collective-permute-start(bf16[3,1,64,256]{3,2,1,0:T(8,128)(2,1)} %get-tuple-element.16), channel_id=1, source_target_pairs={{0,1},{1,2},{2,3},{3,4},{4,5},{5,6},{6,7},{8,9},{9,10},{10,11},{11... | collective-permute-start | bytes 294920 | tf_op jit(solution)/shard_map/ppermute | solution.py:48
  106.9 1.2 copy.29
  108.1 1.5 reshape.119
  109.5 2.0 %collective-permute-start.7 = (bf16[3,1,64,256]{3,2,1,0:T(8,128)(2,1)}, bf16[3,1,64,256]{3,2,1,0:T(8,128)(2,1)S(1)}, u32[]{:S(2)}, u32[]{:S(2)}) collective-permute-start(bf16[3,1,64,256]{3,2,1,0:T(8,128)(2,1)} %get-tuple-element.15), channel_id=1, source_target_pairs={{1,0},{2,1},{3,2},{4,3},{5,4},{6,5},{7,6},{9,8},{10,9},{11,10},{12... | collective-permute-start | bytes 294920 | tf_op jit(solution)/shard_map/ppermute | solution.py:49
  111.7 6.8 %collective-permute-done.7 = bf16[3,1,64,256]{3,2,1,0:T(8,128)(2,1)S(1)} collective-permute-done((bf16[3,1,64,256]{3,2,1,0:T(8,128)(2,1)}, bf16[3,1,64,256]{3,2,1,0:T(8,128)(2,1)S(1)}, u32[]{:S(2)}, u32[]{:S(2)}) %collective-permute-start.7) | collective-permute-done | bytes 98336 | tf_op jit(solution)/shard_map/ppermute | solution.py:49
  119.0 2.6 %fusion.16 = f32[1,32,192,256]{3,2,1,0:T(8,128)S(1)} fusion(bf16[192,576,1]{1,0,2:T(8,128)(2,1)S(1)} %reshape.119, bf16[1,32,576,256]{3,2,1,0:T(8,128)(2,1)S(1)} %fusion.45), kind=kOutput, calls=%fused_computation.20 | convolution fusion | flops 1811939328 | bytes 15949824 | tf_op jit(solution)/shard_map/km,frmn->frkn/dot_general | solution.py:145
  121.6 0.7 fusion.80
  122.4 0.8 fusion.23
  123.2 2.7 %collective-permute-start.8 = (bf16[1,32,64,256]{3,2,1,0:T(8,128)(2,1)S(1)}, bf16[1,32,64,256]{3,2,1,0:T(8,128)(2,1)S(1)}, u32[]{:S(2)}, u32[]{:S(2)}) collective-permute-start(bf16[1,32,64,256]{3,2,1,0:T(8,128)(2,1)S(1)} %fusion.23), channel_id=1, source_target_pairs={{0,8},{8,16},{16,24},{24,32},{32,40},{40,48},{48,56},{56,64},{64,7... | collective-permute-start | bytes 3145736 | tf_op jit(solution)/shard_map/ppermute | solution.py:48
  125.9 5.9 %collective-permute-start.9 = (bf16[1,32,64,256]{3,2,1,0:T(8,128)(2,1)S(1)}, bf16[1,32,64,256]{3,2,1,0:T(8,128)(2,1)S(1)}, u32[]{:S(2)}, u32[]{:S(2)}) collective-permute-start(bf16[1,32,64,256]{3,2,1,0:T(8,128)(2,1)S(1)} %fusion.23), channel_id=1, source_target_pairs={{8,0},{16,8},{24,16},{32,24},{40,32},{48,40},{56,48},{64,56},{72,6... | collective-permute-start | bytes 3145736 | tf_op jit(solution)/shard_map/ppermute | solution.py:49
  131.8 14.1 %collective-permute-done.8 = bf16[1,32,64,256]{3,2,1,0:T(8,128)(2,1)S(1)} collective-permute-done((bf16[1,32,64,256]{3,2,1,0:T(8,128)(2,1)S(1)}, bf16[1,32,64,256]{3,2,1,0:T(8,128)(2,1)S(1)}, u32[]{:S(2)}, u32[]{:S(2)}) %collective-permute-start.8) | collective-permute-done | bytes 1048608 | tf_op jit(solution)/shard_map/ppermute | solution.py:48
  145.9 4.2 %collective-permute-done.9 = bf16[1,32,64,256]{3,2,1,0:T(8,128)(2,1)S(1)} collective-permute-done((bf16[1,32,64,256]{3,2,1,0:T(8,128)(2,1)S(1)}, bf16[1,32,64,256]{3,2,1,0:T(8,128)(2,1)S(1)}, u32[]{:S(2)}, u32[]{:S(2)}) %collective-permute-start.9) | collective-permute-done | bytes 1048608 | tf_op jit(solution)/shard_map/ppermute | solution.py:49
  150.1 5.9 %collective-permute-start.10 = (bf16[3,1,64,256]{3,2,1,0:T(8,128)(2,1)S(1)}, bf16[3,1,64,256]{3,2,1,0:T(8,128)(2,1)S(1)}, u32[]{:S(2)}, u32[]{:S(2)}) collective-permute-start(bf16[3,1,64,256]{3,2,1,0:T(8,128)(2,1)S(1)} %get-tuple-element.14), channel_id=1, source_target_pairs={{0,1},{1,2},{2,3},{3,4},{4,5},{5,6},{6,7},{8,9},{9,10},{10,11},{11... | collective-permute-start | bytes 294920 | tf_op jit(solution)/shard_map/ppermute | solution.py:48
  156.1 1.9 %collective-permute-start.11 = (bf16[3,1,64,256]{3,2,1,0:T(8,128)(2,1)S(1)}, bf16[3,1,64,256]{3,2,1,0:T(8,128)(2,1)S(1)}, u32[]{:S(2)}, u32[]{:S(2)}) collective-permute-start(bf16[3,1,64,256]{3,2,1,0:T(8,128)(2,1)S(1)} %get-tuple-element.13), channel_id=1, source_target_pairs={{1,0},{2,1},{3,2},{4,3},{5,4},{6,5},{7,6},{9,8},{10,9},{11,10},{12... | collective-permute-start | bytes 294920 | tf_op jit(solution)/shard_map/ppermute | solution.py:49
  158.3 6.4 %collective-permute-done.11 = bf16[3,1,64,256]{3,2,1,0:T(8,128)(2,1)S(1)} collective-permute-done((bf16[3,1,64,256]{3,2,1,0:T(8,128)(2,1)S(1)}, bf16[3,1,64,256]{3,2,1,0:T(8,128)(2,1)S(1)}, u32[]{:S(2)}, u32[]{:S(2)}) %collective-permute-start.11) | collective-permute-done | bytes 98336 | tf_op jit(solution)/shard_map/ppermute | solution.py:49
  165.3 1.3 fusion.38
  167.0 0.6 fusion.74
  (70 shorter events, 4.1 us)
Async XLA Ops:
  1.6 14.8 %all-to-all-start = ((bf16[8,1,32,512]{3,2,1,0:T(8,128)(2,1)}), bf16[8,1,32,512]{3,2,1,0:T(8,128)(2,1)S(1)}, u32[]{:S(2)}, u32[]{:S(2)}) async-start(bf16[8,1,32,512]{3,2,1,0:T(8,128)(2,1)} %broadcast_in_dim.12), calls=%async_computation | async-start | bytes 524288 | tf_op jit(solution)/shard_map/all_to_all | solution.py:13
  8.7 4.1 %copy-start.11 = (s32[1,8,256]{2,1,0:T(8,128)S(1)}, s32[1,8,256]{2,1,0:T(8,128)}, u32[]{:S(2)}) copy-start(s32[1,8,256]{2,1,0:T(8,128)} %param.11) | copy-start | bytes 24580
  8.7 5.1 %copy-start.1 = (bf16[8,256,512]{2,1,0:T(8,128)(2,1)S(1)}, bf16[8,256,512]{2,1,0:T(8,128)(2,1)}, u32[]{:S(2)}) copy-start(bf16[8,256,512]{2,1,0:T(8,128)(2,1)} %param.10) | copy-start | bytes 6291460
  20.6 1.7 %copy-start.4 = (bf16[1,8,256,512]{3,2,1,0:T(8,128)(2,1)}, bf16[1,8,256,512]{3,2,1,0:T(8,128)(2,1)S(1)}, u32[]{:S(2)}) copy-start(bf16[1,8,256,512]{3,2,1,0:T(8,128)(2,1)S(1)} %convert_bitcast_fusion.1) | copy-start | bytes 6291460
  20.6 2.7 %copy-start.2 = (bf16[1,8,256,512]{2,3,1,0:T(8,128)(2,1)S(1)}, bf16[1,8,256,512]{2,3,1,0:T(8,128)(2,1)}, u32[]{:S(2)}) copy-start(bf16[1,8,256,512]{2,3,1,0:T(8,128)(2,1)} %copy.24) | copy-start | bytes 6291460
  31.0 2.2 %copy-start.3 = (bf16[1,8,256,512]{3,2,1,0:T(8,128)(2,1)S(1)}, bf16[1,8,256,512]{3,2,1,0:T(8,128)(2,1)}, u32[]{:S(2)}) copy-start(bf16[1,8,256,512]{3,2,1,0:T(8,128)(2,1)} %convert_bitcast_fusion) | copy-start | bytes 6291460
  33.2 2.2 %copy-start = (f32[1,8,256,512]{3,2,1,0:T(8,128)S(1)}, f32[1,8,256,512]{3,2,1,0:T(8,128)}, u32[]{:S(2)}) copy-start(f32[1,8,256,512]{3,2,1,0:T(8,128)} %bitcast_convert_fusion) | copy-start | bytes 12582916
  36.1 12.9 %copy-start.5 = (f32[1,32,512]{2,1,0:T(8,128)S(1)}, f32[1,32,512]{2,1,0:T(8,128)}, u32[]{:S(2)}) copy-start(f32[1,32,512]{2,1,0:T(8,128)} %param.12) | copy-start | bytes 196612
  36.1 29.7 %copy-start.9 = (bf16[3,3,3,64,2]{3,4,2,1,0:T(2,128)(2,1)S(1)}, bf16[3,3,3,64,2]{3,4,2,1,0:T(2,128)(2,1)}, u32[]{:S(2)}) copy-start(bf16[3,3,3,64,2]{3,4,2,1,0:T(2,128)(2,1)} %param.13) | copy-start | bytes 20740
  49.0 23.9 %copy-start.6 = (f32[32,512]{1,0:T(8,128)}, f32[32,512]{1,0:T(8,128)S(1)}, u32[]{:S(2)}) copy-start(f32[32,512]{1,0:T(8,128)S(1)} %reduce_sum.19) | copy-start | bytes 196612
  49.0 8.6 %collective-permute-start = (bf16[1,32,2,256]{3,2,1,0:T(2,128)(2,1)S(1)}, bf16[1,32,2,256]{3,2,1,0:T(2,128)(2,1)S(1)}, u32[]{:S(2)}, u32[]{:S(2)}) collective-permute-start(bf16[1,32,2,256]{3,2,1,0:T(2,128)(2,1)S(1)} %convert_element_type.117), channel_id=1, source_target_pairs={{0,8},{8,16},{16,24},{24,32},{32,40},{40,48},{48,56},{56,64},{64,7... | collective-permute-start | bytes 98312 | tf_op jit(solution)/shard_map/ppermute | solution.py:48
  50.9 8.2 %collective-permute-start.1 = (bf16[1,32,2,256]{3,2,1,0:T(2,128)(2,1)S(1)}, bf16[1,32,2,256]{3,2,1,0:T(2,128)(2,1)S(1)}, u32[]{:S(2)}, u32[]{:S(2)}) collective-permute-start(bf16[1,32,2,256]{3,2,1,0:T(2,128)(2,1)S(1)} %convert_element_type.117), channel_id=1, source_target_pairs={{8,0},{16,8},{24,16},{32,24},{40,32},{48,40},{56,48},{64,56},{72,6... | collective-permute-start | bytes 98312 | tf_op jit(solution)/shard_map/ppermute | solution.py:49
  59.2 6.6 %collective-permute-start.2 = (bf16[3,1,2,256]{3,2,1,0:T(2,128)(2,1)S(1)}, bf16[3,1,2,256]{3,2,1,0:T(2,128)(2,1)S(1)}, u32[]{:S(2)}, u32[]{:S(2)}) collective-permute-start(bf16[3,1,2,256]{3,2,1,0:T(2,128)(2,1)S(1)} %get-tuple-element.35), channel_id=1, source_target_pairs={{0,1},{1,2},{2,3},{3,4},{4,5},{5,6},{6,7},{8,9},{9,10},{10,11},{11... | collective-permute-start | bytes 9224 | tf_op jit(solution)/shard_map/ppermute | solution.py:48
  63.6 7.6 %collective-permute-start.3 = (bf16[3,1,2,256]{3,2,1,0:T(2,128)(2,1)S(1)}, bf16[3,1,2,256]{3,2,1,0:T(2,128)(2,1)S(1)}, u32[]{:S(2)}, u32[]{:S(2)}) collective-permute-start(bf16[3,1,2,256]{3,2,1,0:T(2,128)(2,1)S(1)} %get-tuple-element.34), channel_id=1, source_target_pairs={{1,0},{2,1},{3,2},{4,3},{5,4},{6,5},{7,6},{9,8},{10,9},{11,10},{12... | collective-permute-start | bytes 9224 | tf_op jit(solution)/shard_map/ppermute | solution.py:49
  72.8 0.8 copy-start.12
  74.4 32.5 %copy-start.8 = (bf16[3,3,3,64,64]{4,3,2,1,0:T(8,128)(2,1)S(1)}, bf16[3,3,3,64,64]{4,3,2,1,0:T(8,128)(2,1)}, u32[]{:S(2)}) copy-start(bf16[3,3,3,64,64]{4,3,2,1,0:T(8,128)(2,1)} %param.15) | copy-start | bytes 663556
  74.4 26.3 %collective-permute-start.4 = (bf16[1,32,64,256]{3,2,1,0:T(8,128)(2,1)S(1)}, bf16[1,32,64,256]{3,2,1,0:T(8,128)(2,1)S(1)}, u32[]{:S(2)}, u32[]{:S(2)}) collective-permute-start(bf16[1,32,64,256]{3,2,1,0:T(8,128)(2,1)S(1)} %fusion.27), channel_id=1, source_target_pairs={{0,8},{8,16},{16,24},{24,32},{32,40},{40,48},{48,56},{56,64},{64,7... | collective-permute-start | bytes 3145736 | tf_op jit(solution)/shard_map/ppermute | solution.py:48
  76.6 25.7 %collective-permute-start.5 = (bf16[1,32,64,256]{3,2,1,0:T(8,128)(2,1)S(1)}, bf16[1,32,64,256]{3,2,1,0:T(8,128)(2,1)S(1)}, u32[]{:S(2)}, u32[]{:S(2)}) collective-permute-start(bf16[1,32,64,256]{3,2,1,0:T(8,128)(2,1)S(1)} %fusion.27), channel_id=1, source_target_pairs={{8,0},{16,8},{24,16},{32,24},{40,32},{48,40},{56,48},{64,56},{72,6... | collective-permute-start | bytes 3145736 | tf_op jit(solution)/shard_map/ppermute | solution.py:49
  103.0 8.5 %collective-permute-start.6 = (bf16[3,1,64,256]{3,2,1,0:T(8,128)(2,1)}, bf16[3,1,64,256]{3,2,1,0:T(8,128)(2,1)S(1)}, u32[]{:S(2)}, u32[]{:S(2)}) collective-permute-start(bf16[3,1,64,256]{3,2,1,0:T(8,128)(2,1)} %get-tuple-element.16), channel_id=1, source_target_pairs={{0,1},{1,2},{2,3},{3,4},{4,5},{5,6},{6,7},{8,9},{9,10},{10,11},{11... | collective-permute-start | bytes 294920 | tf_op jit(solution)/shard_map/ppermute | solution.py:48
  109.5 8.9 %collective-permute-start.7 = (bf16[3,1,64,256]{3,2,1,0:T(8,128)(2,1)}, bf16[3,1,64,256]{3,2,1,0:T(8,128)(2,1)S(1)}, u32[]{:S(2)}, u32[]{:S(2)}) collective-permute-start(bf16[3,1,64,256]{3,2,1,0:T(8,128)(2,1)} %get-tuple-element.15), channel_id=1, source_target_pairs={{1,0},{2,1},{3,2},{4,3},{5,4},{6,5},{7,6},{9,8},{10,9},{11,10},{12... | collective-permute-start | bytes 294920 | tf_op jit(solution)/shard_map/ppermute | solution.py:49
  121.6 0.8 copy-start.13
  123.2 32.8 %copy-start.10 = (bf16[3,3,3,2,64]{4,3,2,1,0:T(2,128)(2,1)S(1)}, bf16[3,3,3,2,64]{4,3,2,1,0:T(2,128)(2,1)}, u32[]{:S(2)}) copy-start(bf16[3,3,3,2,64]{4,3,2,1,0:T(2,128)(2,1)} %param.17) | copy-start | bytes 20740
  123.2 22.6 %collective-permute-start.8 = (bf16[1,32,64,256]{3,2,1,0:T(8,128)(2,1)S(1)}, bf16[1,32,64,256]{3,2,1,0:T(8,128)(2,1)S(1)}, u32[]{:S(2)}, u32[]{:S(2)}) collective-permute-start(bf16[1,32,64,256]{3,2,1,0:T(8,128)(2,1)S(1)} %fusion.23), channel_id=1, source_target_pairs={{0,8},{8,16},{16,24},{24,32},{32,40},{40,48},{48,56},{56,64},{64,7... | collective-permute-start | bytes 3145736 | tf_op jit(solution)/shard_map/ppermute | solution.py:48
  125.9 24.2 %collective-permute-start.9 = (bf16[1,32,64,256]{3,2,1,0:T(8,128)(2,1)S(1)}, bf16[1,32,64,256]{3,2,1,0:T(8,128)(2,1)S(1)}, u32[]{:S(2)}, u32[]{:S(2)}) collective-permute-start(bf16[1,32,64,256]{3,2,1,0:T(8,128)(2,1)S(1)} %fusion.23), channel_id=1, source_target_pairs={{8,0},{16,8},{24,16},{32,24},{40,32},{48,40},{56,48},{64,56},{72,6... | collective-permute-start | bytes 3145736 | tf_op jit(solution)/shard_map/ppermute | solution.py:49
  150.1 8.1 %collective-permute-start.10 = (bf16[3,1,64,256]{3,2,1,0:T(8,128)(2,1)S(1)}, bf16[3,1,64,256]{3,2,1,0:T(8,128)(2,1)S(1)}, u32[]{:S(2)}, u32[]{:S(2)}) collective-permute-start(bf16[3,1,64,256]{3,2,1,0:T(8,128)(2,1)S(1)} %get-tuple-element.14), channel_id=1, source_target_pairs={{0,1},{1,2},{2,3},{3,4},{4,5},{5,6},{6,7},{8,9},{9,10},{10,11},{11... | collective-permute-start | bytes 294920 | tf_op jit(solution)/shard_map/ppermute | solution.py:48
  156.1 8.6 %collective-permute-start.11 = (bf16[3,1,64,256]{3,2,1,0:T(8,128)(2,1)S(1)}, bf16[3,1,64,256]{3,2,1,0:T(8,128)(2,1)S(1)}, u32[]{:S(2)}, u32[]{:S(2)}) collective-permute-start(bf16[3,1,64,256]{3,2,1,0:T(8,128)(2,1)S(1)} %get-tuple-element.13), channel_id=1, source_target_pairs={{1,0},{2,1},{3,2},{4,3},{5,4},{6,5},{7,6},{9,8},{10,9},{11,10},{12... | collective-permute-start | bytes 294920 | tf_op jit(solution)/shard_map/ppermute | solution.py:49
  165.3 1.7 %copy-start.7 = (f32[32,512]{1,0:T(8,128)S(1)}, f32[32,512]{1,0:T(8,128)}, u32[]{:S(2)}) copy-start(f32[32,512]{1,0:T(8,128)} %copy-done.6) | copy-start | bytes 196612
where the time goes:
time: 169 us; the launch traced here: 168 us
  waiting for transfers between devices  57.6 us (34%)
  starting transfers between devices  52 us (31%)
  other arithmetic  16.4 us (10%)
  matrix products  15.2 us (9%)
  local copies, waits for them, and re-layouts  13.3 us (8%)
  blocking collectives  12.5 us (7%)
    ppermute x6, waiting for transfers between devices, with_halo(): before = lax.ppermute(last, axis, up)  31.8 us
    ppermute x6, waiting for transfers between devices, with_halo(): after = lax.ppermute(leading, axis, down)  25.8 us
    ppermute x6, starting transfers between devices, with_halo(): after = lax.ppermute(leading, axis, down)  25.1 us
    ppermute x6, starting transfers between devices, with_halo(): before = lax.ppermute(last, axis, up)  20.9 us
    all_to_all x1, blocking collectives, sent_and_summed(): lax.all_to_all(parts, axis, split_axis=0, concat_axis=0, tiled=True)  12.5 us
    dot_general x1, matrix products, data_step(): jnp.einsum('fckm,mn->fckn', misfit, behind, preferred_element_type=f32)  7.7 us
    unnamed x37, local copies, waits for them, and re-layouts  7.49 us
    all_to_all x1, starting transfers between devices, from_everyone(): lax.all_to_all(jnp.broadcast_to(shard[None], (devices, *shard.shape)), ax...  6.04 us
  transfers between devices with their start and end apart: 13, of which 9 were waited for; matrix products, arithmetic and copies ran while one was open for 7% of the time, Pallas kernels for 0%

commit v1 on v0

v1 whole, which is shorter than its diff:
```python
import functools

import jax
import jax.numpy as jnp
import numpy as np
from jax import lax
from jax.experimental import pallas as pl
from jax.experimental.pallas import tpu as pltpu
from jax.sharding import PartitionSpec as P

F32 = jnp.float32
BF16 = jnp.bfloat16
MESH = pl.DeviceIdType.MESH

ROWS = 256
N = 256
RB = 32
HR = 48
NCO = 8
CH = 64
GRP = 8


def dft_tables():
    idx = np.arange(N)
    ang = (idx[:, None] * idx[None, :] % N) * (2.0 * np.pi / N)
    fr = (np.cos(ang) / np.sqrt(N)).astype(np.float32)
    fi = (-np.sin(ang) / np.sqrt(N)).astype(np.float32)
    cols = np.block([[fr, fi], [-fi, fr]])
    back = np.block([[fr, -fi], [fi, fr]])
    rows = np.block([[fr, -fi], [fi, fr]])
    rback = np.block([[fr, fi], [-fi, fr]])
    return cols, back, rows, rback


def shift_right(v):
    lane = lax.broadcasted_iota(jnp.int32, v.shape, 1)
    return jnp.where(lane == 0, 0.0, pltpu.roll(v, 1, axis=1))


def shift_left(v):
    lane = lax.broadcasted_iota(jnp.int32, v.shape, 1)
    return jnp.where(lane == N - 1, 0.0, pltpu.roll(v, N - 1, axis=1))


def dot(a, b):
    return jnp.dot(a, b, preferred_element_type=F32)


def kernel(
    frames,
    kspace_hbm, sens_hbm, mask_hbm, image_hbm, ta_hbm, tb_hbm, w1_hbm, w2_hbm, w3_hbm, b1_hbm, b2_hbm,
    out_ref,
    ksp, sens, mask, image, ta, tb, w1, w2, w3, b1, b2,
    xb, ci, cols, acc, gs, grecv, xr, x48, hb, kb, h1, h2, psend, precv,
    lsem, asend, arecv, bsend, brecv, csend, crecv, dsend, drecv,
):
    t = lax.axis_index("frame")
    j = lax.axis_index("coil")
    r0 = pl.multiple_of(j * RB, RB)

    loads = [
        pltpu.make_async_copy(src, dst, lsem.at[i])
        for i, (src, dst) in enumerate(
            [
                (image_hbm, image), (sens_hbm, sens), (ta_hbm, ta), (tb_hbm, tb), (kspace_hbm, ksp),
                (mask_hbm, mask), (w1_hbm, w1), (w2_hbm, w2), (w3_hbm, w3), (b1_hbm, b1), (b2_hbm, b2),
            ]
        )
    ]
    for c in loads:
        c.start()

    partners = [(d, (t + d >= 0) & (t + d < frames)) for d in (-2, -1, 1, 2)]

    barrier = pltpu.get_barrier_semaphore()
    for s in range(1, GRP):
        pl.semaphore_signal(barrier, inc=1, device_id={"coil": lax.rem(j + s, GRP)}, device_id_type=MESH)
    for d, here in partners:
        @pl.when(here)
        def _():
            pl.semaphore_signal(barrier, inc=1, device_id={"frame": t + d}, device_id_type=MESH)

    loads[0].wait()
    xb[pl.ds(r0, RB), :] = image[...].astype(BF16)
    present = sum(here.astype(jnp.int32) for _, here in partners)
    pl.semaphore_wait(barrier, GRP - 1 + present)

    acopy = []
    for s in range(1, GRP):
        c = pltpu.make_async_remote_copy(
            src_ref=xb.at[pl.ds(r0, RB)],
            dst_ref=xb.at[pl.ds(r0, RB)],
            send_sem=asend.at[s],
            recv_sem=arecv.at[s],
            device_id={"coil": lax.rem(j + s, GRP)},
            device_id_type=MESH,
        )
        c.start()
        acopy.append(c)

    loads[1].wait()
    loads[2].wait()

    def columns(q):
        rq = pl.multiple_of(q * RB, RB)
        xv = xb[pl.ds(rq, RB), :].astype(F32)
        x_re, x_im = xv[:, :N], xv[:, N:]
        for c in range(NCO):
            sv = sens[c, pl.ds(rq, RB), :].astype(F32)
            s_re, s_im = sv[:, :N], sv[:, N:]
            ci[c * RB : (c + 1) * RB, :N] = (s_re * x_re - s_im * x_im).astype(BF16)
            ci[c * RB : (c + 1) * RB, N:] = (s_re * x_im + s_im * x_re).astype(BF16)
        for half in range(2):
            spec = dot(ci[...], ta[0, :, half * N : (half + 1) * N]).astype(BF16)
            for c in range(NCO):
                cols[c, pl.ds(half * ROWS + rq, RB), :] = spec[c * RB : (c + 1) * RB]

    columns(j)

    @pl.loop(1, GRP)
    def _(s):
        pltpu.make_async_remote_copy(
            src_ref=xb.at[pl.ds(r0, RB)],
            dst_ref=xb.at[pl.ds(pl.multiple_of(lax.rem(j - s + GRP, GRP) * RB, RB), RB)],
            send_sem=asend.at[s],
            recv_sem=arecv.at[s],
            device_id={"coil": lax.rem(j + s, GRP)},
            device_id_type=MESH,
        ).wait_recv()
        columns(lax.rem(j - s + GRP, GRP))

    loads[3].wait()
    loads[4].wait()
    loads[5].wait()

    def coil(c):
        halves = []
        for half in range(2):
            est = dot(tb[0, half * ROWS : (half + 1) * ROWS, :], cols[c])
            k = ksp[c, :, half * N : (half + 1) * N].astype(F32)
            halves.append((est - k).astype(BF16))
        misfit = jnp.concatenate(halves, axis=1)
        stacked = jnp.concatenate(
            [dot(misfit, ta[1, :, half * N : (half + 1) * N]).astype(BF16) for half in range(2)], axis=0
        )
        m = mask[pl.ds(c, 1), :].astype(F32).astype(BF16)
        mm = jnp.concatenate([m, m], axis=1)
        b_re = dot(tb[1, :ROWS, :] * mm, stacked)
        b_im = dot(tb[1, ROWS:, :] * mm, stacked)
        s_re, s_im = sens[c, :, :N].astype(F32), sens[c, :, N:].astype(F32)
        return s_re * b_re + s_im * b_im, s_re * b_im - s_im * b_re

    first_re, first_im = coil(0)
    acc[:, :N] = first_re
    acc[:, N:] = first_im

    @pl.loop(1, NCO)
    def _(c):
        g_re, g_im = coil(c)
        acc[:, :N] += g_re
        acc[:, N:] += g_im

    gs[:ROWS, :] = pltpu.roll(acc[...], 3, axis=0).astype(BF16)
    gs[ROWS : ROWS + 16, :] = pltpu.roll(acc[ROWS - 16 :, :], 3, axis=0).astype(BF16)

    bcopy = []
    for s in range(1, GRP):
        to = lax.rem(j + s, GRP)
        c = pltpu.make_async_remote_copy(
            src_ref=gs.at[pl.ds(pl.multiple_of(to * RB, RB), HR)],
            dst_ref=grecv.at[s],
            send_sem=bsend.at[s],
            recv_sem=brecv.at[s],
            device_id={"coil": to},
            device_id_type=MESH,
        )
        c.start()
        bcopy.append(c)

    xr[:ROWS, :] = pltpu.roll(xb[...].astype(F32), 3, axis=0)
    xr[ROWS : ROWS + 16, :] = jnp.zeros((16, 2 * N), F32)
    x48[...] = xr[pl.ds(r0, HR), :]
    x48[3 : 3 + RB, :] = image[...]
    for c in loads[6:]:
        c.wait()
    total = x48[...] - gs[pl.ds(r0, HR), :].astype(F32)
    for c in bcopy:
        c.wait_recv()
    for s in range(1, GRP):
        total = total - grecv[s].astype(F32)
    row = r0 - 3 + lax.broadcasted_iota(jnp.int32, (HR, 2 * N), 0)
    total = jnp.where((row >= 0) & (row < ROWS), total, 0.0)
    x48[...] = total
    hb[2] = total.astype(BF16)

    for d, here in partners:
        def ccopy(d=d):
            return pltpu.make_async_remote_copy(
                src_ref=hb.at[2],
                dst_ref=hb.at[2 - d],
                send_sem=csend.at[d + 2],
                recv_sem=crecv.at[d + 2],
                device_id={"frame": t + d},
                device_id_type=MESH,
            )

        @pl.when(here)
        def _():
            ccopy().start()

        @pl.when(jnp.logical_not(here))
        def _():
            hb[2 + d] = jnp.zeros((HR, 2 * N), BF16)

    def planes(f):
        v = hb[f].astype(F32)
        parts = []
        for half in range(2):
            p = v[:, half * N : (half + 1) * N]
            parts += [shift_right(p), p, shift_left(p)]
        for i in range(HR // 8):
            kb[i, f * HR : (f + 1) * HR, :] = jnp.concatenate(
                [p[8 * i : 8 * i + 8] for p in parts], axis=0
            ).astype(BF16)

    planes(2)
    for d, here in partners:
        @pl.when(here)
        def _():
            pltpu.make_async_remote_copy(
                src_ref=hb.at[2],
                dst_ref=hb.at[2 + d],
                send_sem=csend.at[2 - d],
                recv_sem=crecv.at[2 - d],
                device_id={"frame": t + d},
                device_id_type=MESH,
            ).wait_recv()

        planes(2 + d)

    bias1 = b1[...]
    for f in range(3):
        @pl.loop(0, 5)
        def _(i):
            here_k = kb[i, f * HR : (f + 3) * HR, :]
            next_k = kb[i + 1, f * HR : (f + 3) * HR, :]
            top = dot(w1[:384, :], here_k)
            low = dot(w1[384:512, :], here_k) + dot(w1[512:, :], next_k)
            base = pl.multiple_of(i * 512, 512)
            for q in range(6):
                h1[f, pl.ds(base + q * CH, CH), :] = jnp.maximum(top[q * CH : (q + 1) * CH] + bias1, 0.0).astype(BF16)
            for q in range(2):
                h1[f, pl.ds(base + (6 + q) * CH, CH), :] = jnp.maximum(low[q * CH : (q + 1) * CH] + bias1, 0.0).astype(BF16)

    @pl.when(j == 0)
    def _():
        h1[:, : 2 * CH, :] = jnp.zeros((3, 2 * CH, N), BF16)

    @pl.when(j == GRP - 1)
    def _():
        h1[:, 34 * CH :, :] = jnp.zeros((3, 6 * CH, N), BF16)

    @pl.when(t == 0)
    def _():
        h1[0] = jnp.zeros((40 * CH, N), BF16)

    @pl.when(t == frames - 1)
    def _():
        h1[2] = jnp.zeros((40 * CH, N), BF16)

    bias2 = b2[...]

    @pl.loop(0, 17)
    def _(i):
        for q in range(2):
            base = pl.multiple_of((2 * i + q) * CH, CH)
            taps = dot(w2[0], h1[0, pl.ds(base, 3 * CH), :])
            taps += dot(w2[1], h1[1, pl.ds(base, 3 * CH), :])
            taps += dot(w2[2], h1[2, pl.ds(base, 3 * CH), :])
            v = taps[CH : 2 * CH] + shift_right(taps[:CH]) + shift_left(taps[2 * CH :]) + bias2
            h2[pl.ds(base, CH), :] = jnp.maximum(v, 0.0).astype(BF16)

    @pl.when(j == 0)
    def _():
        h2[:CH, :] = jnp.zeros((CH, N), BF16)

    @pl.when(j == GRP - 1)
    def _():
        h2[33 * CH :, :] = jnp.zeros((CH, N), BF16)

    @pl.loop(0, RB // 8)
    def _(i):
        base = pl.multiple_of(i * 8 * CH, 8 * CH)
        taps = dot(w3[...], h2[pl.ds(base, 10 * CH), :])
        v = taps[48:96] + shift_right(taps[:48]) + shift_left(taps[96:])
        ri = pl.multiple_of(i * 8, 8)
        for a in range(3):
            for half in range(2):
                o = (a * 2 + half) * 8
                psend[a, pl.ds(ri, 8), half * N : (half + 1) * N] = v[o : o + 8]

    ends = [(1, 0, t + 1 < frames), (-1, 2, t >= 1)]
    for n, (d, a, here) in enumerate(ends):
        @pl.when(here)
        def _():
            pltpu.make_async_remote_copy(
                src_ref=psend.at[a],
                dst_ref=precv.at[n],
                send_sem=dsend.at[n],
                recv_sem=drecv.at[n],
                device_id={"frame": t + d},
                device_id_type=MESH,
            ).start()

    out_ref[...] = x48[3 : 3 + RB, :] + psend[1]
    for n, (d, a, here) in enumerate(ends):
        @pl.when((t - d >= 0) & (t - d < frames))
        def _():
            pltpu.make_async_remote_copy(
                src_ref=psend.at[a],
                dst_ref=precv.at[n],
                send_sem=dsend.at[n],
                recv_sem=drecv.at[n],
                device_id={"frame": t - d},
                device_id_type=MESH,
            ).wait_recv()
            out_ref[...] += precv[n]

    for c in acopy + bcopy:
        c.wait_send()
    for d, here in partners:
        @pl.when(here)
        def _():
            pltpu.make_async_remote_copy(
                src_ref=hb.at[2],
                dst_ref=hb.at[2 - d],
                send_sem=csend.at[d + 2],
                recv_sem=crecv.at[d + 2],
                device_id={"frame": t + d},
                device_id_type=MESH,
            ).wait_send()
    for n, (d, a, here) in enumerate(ends):
        @pl.when(here)
        def _():
            pltpu.make_async_remote_copy(
                src_ref=psend.at[a],
                dst_ref=precv.at[n],
                send_sem=dsend.at[n],
                recv_sem=drecv.at[n],
                device_id={"frame": t + d},
                device_id_type=MESH,
            ).wait_send()


def spread(rows, width, first):
    out = np.zeros((3, rows, width), np.float32)
    for q in range(rows):
        for b in range(3):
            u = q + first + b
            if 0 <= u < width:
                out[b, q, u] = 1
    return out


def shards(frames, kspace, sens, mask, image, w_first, b_first, w_mid, b_mid, w_last):
    cols, back, rows, rback = dft_tables()
    ta = jnp.asarray(np.stack([cols, back]), BF16)
    tb = jnp.asarray(np.stack([rows, rback]), BF16)
    here = spread(8, 8, 0)
    ahead = spread(2, 8, -2)
    pick1 = jnp.asarray(np.concatenate([here, ahead], axis=1), BF16)
    w1 = jnp.einsum("abeoc,bqu->qoaceu", w_first, pick1).reshape(10 * CH, 3 * HR)
    w2 = jnp.transpose(w_mid, (0, 2, 3, 1, 4)).reshape(3, 3 * CH, 3 * CH)
    pick3 = jnp.asarray(spread(8, 10, 0), BF16)
    w3 = jnp.einsum("abeoi,bqu->eaoqui", w_last, pick3).reshape(144, 10 * CH)
    b1 = jnp.broadcast_to(b_first[:, None], (CH, N))
    b2 = jnp.broadcast_to(b_mid[:, None], (CH, N))
    args = (kspace[0], sens, mask[0], image[0], ta, tb, w1, w2, w3, b1, b2)
    order = args
    dma = pltpu.SemaphoreType.DMA
    out = pl.pallas_call(
        functools.partial(kernel, frames),
        out_shape=jax.ShapeDtypeStruct((RB, 2 * N), F32),
        in_specs=[pl.BlockSpec(memory_space=pl.ANY)] * len(args),
        out_specs=pl.BlockSpec(memory_space=pltpu.VMEM),
        scratch_shapes=[pltpu.VMEM(a.shape, a.dtype) for a in order]
        + [
            pltpu.VMEM((ROWS, 2 * N), BF16),
            pltpu.VMEM((NCO * RB, 2 * N), BF16),
            pltpu.VMEM((NCO, 2 * ROWS, N), BF16),
            pltpu.VMEM((ROWS, 2 * N), F32),
            pltpu.VMEM((ROWS + 16, 2 * N), BF16),
            pltpu.VMEM((GRP, HR, 2 * N), BF16),
            pltpu.VMEM((ROWS + 16, 2 * N), F32),
            pltpu.VMEM((HR, 2 * N), F32),
            pltpu.VMEM((5, HR, 2 * N), BF16),
            pltpu.VMEM((HR // 8, 5 * HR, N), BF16),
            pltpu.VMEM((3, 40 * CH, N), BF16),
            pltpu.VMEM((34 * CH, N), BF16),
            pltpu.VMEM((3, RB, 2 * N), F32),
            pltpu.VMEM((2, RB, 2 * N), F32),
            dma((len(args),)), dma((GRP,)), dma((GRP,)), dma((GRP,)), dma((GRP,)),
            dma((5,)), dma((5,)), dma((2,)), dma((2,)),
        ],
        compiler_params=pltpu.CompilerParams(
            collective_id=0, has_side_effects=True, vmem_limit_bytes=56 * 1024 * 1024
        ),
    )(*args)
    return out[None]


def solution(mesh):
    in_specs = (
        P("frame", "coil", None, None),
        P("coil", None, None),
        P("frame", "coil", None),
        P("frame", "coil", None),
        P(),
        P(),
        P(),
        P(),
        P(),
    )
    out_specs = P("frame", "coil", None)
    body = functools.partial(shards, mesh.shape["frame"])
    return jax.shard_map(body, mesh=mesh, in_specs=in_specs, out_specs=out_specs, check_vma=False)
```

time: 169 us -> 58.2 us (0.34)
  waiting for transfers between devices: 57.6 us -> 0 us
  starting transfers between devices: 52 us -> 0 us
  Pallas kernels: 0 us -> 49.5 us
  other arithmetic: 16.4 us -> 0 us
  matrix products: 15.2 us -> 1.48 us
  blocking collectives: 12.5 us -> 0 us
  local copies, waits for them, and re-layouts: 13.3 us -> 6.93 us
    ppermute x12 -> x0, waiting for transfers between devices: 57.6 us -> none  [the longest x6 31.8 us: with_halo(): before = lax.ppermute(last, axis, up)]
    pallas_call x0 -> x1, Pallas kernels: none -> 49.5 us  [shards(): pl.pallas_call(functools.partial(kernel, frames), out_shape=jax.ShapeDtyp...]
    ppermute x12 -> x0, starting transfers between devices: 46 us -> none  [the longest x6 25.1 us: with_halo(): after = lax.ppermute(leading, axis, down)]
    dot_general x6 -> x2, matrix products: 15.2 us -> 1.48 us  [the longest x1 1.12 us: shards(): jnp.einsum('abeoc,bqu->qoaceu', w_first, pick1).reshape(10 * CH, 3 * HR)]
    all_to_all x1 -> x0, blocking collectives: 12.5 us -> none  [sent_and_summed(): lax.all_to_all(parts, axis, split_axis=0, concat_axis=0, tiled=True)]
    all_to_all x1 -> x0, starting transfers between devices: 6.04 us -> none  [from_everyone(): lax.all_to_all(jnp.broadcast_to(shard[None], (devices, *shard.shape)), ax...]
    unnamed x37 -> x11, local copies, waits for them, and re-layouts: 7.49 us -> 1.5 us
    neg x3 -> x0, other arithmetic: 3.98 us -> none  [the longest x2 2.99 us: swapped(): -values[..., half_width:]]
  transfers between devices with their start and end apart: 13 -> 0, of which waited for: 9 -> 0; matrix products, arithmetic and copies ran while one was open for 7% -> 0% of each run, Pallas kernels for 0% -> 0%
where the time goes in v1:
time: 58.2 us; the launch traced here: 58 us
  Pallas kernels  49.5 us (85%)
  local copies, waits for them, and re-layouts  6.93 us (12%)
  matrix products  1.48 us (3%)
    pallas_call x1, Pallas kernels, shards(): pl.pallas_call(functools.partial(kernel, frames), out_shape=jax.ShapeDtyp...  49.5 us
    unnamed x11, local copies, waits for them, and re-layouts  1.5 us
    reshape x2, local copies, waits for them, and re-layouts, shards(): jnp.einsum('abeoc,bqu->qoaceu', w_first, pick1).reshape(10 * CH, 3 * HR)  1.25 us

profile of v1, /device:TPU:30, one launch (start us, length us, event | category | flops | bytes accessed | tf_op | source)
XLA Modules:
  0.0 58.0 jit_solution(3902841725279203888)
XLA Ops:
  0.0 0.0 copy-start.2
  0.0 0.0 copy-start.1
  0.0 1.1 %convolution_bitcast_fusion.1 = bf16[10,64,3,2,3,8]{1,0,3,4,2,5:T(8,128)(2,1)S(1)} fusion(bf16[3,10,8,1,1,1]{1,0,5,4,3,2:T(4,128)(2,1)} %constant.15, bf16[3,3,3,64,2]{3,4,2,1,0:T(2,128)(2,1)} %param.17), kind=kOutput, calls=%fused_computation.1 | convolution fusion | flops 552960 | bytes 191712 | tf_op jit(solution)/shard_map/abeoc,bqu->qoaceu/dot_general | solution.py:373
  1.1 0.2 copy.20
  1.3 0.0 copy-start
  1.3 0.4 reshape.11
  1.7 0.9 %copy.24.w1_hbm = bf16[640,144]{1,0:T(8,128)(2,1)} copy(bf16[640,144]{0,1:T(8,128)(2,1)S(1)} %reshape.11) | data formatting | bytes 368640 | tf_op jit(solution)/shard_map/reshape | solution.py:373
  2.6 0.0 copy-done.2
  2.6 0.0 copy-done.1
  2.6 0.0 copy-start.3
  2.6 0.4 convolution_bitcast_fusion
  2.9 0.0 copy-start.4
  3.0 0.2 copy.23
  3.1 1.0 %reshape.13.w3_hbm = bf16[144,640]{1,0:T(8,128)(2,1)} reshape(bf16[3,3,2,8,10,64]{5,4,3,2,1,0:T(8,128)(2,1)S(1)} %copy.23) | data formatting | bytes 368640 | tf_op jit(solution)/shard_map/reshape | solution.py:376
  4.1 0.0 copy-done
  4.1 0.4 copy.21
  4.5 1.1 %reshape.12.w2_hbm = bf16[3,192,192]{2,1,0:T(8,128)(2,1)} reshape(bf16[3,3,64,3,64]{4,3,2,1,0:T(4,128)(2,1)S(1)} %copy.21) | data formatting | bytes 442368 | tf_op jit(solution)/shard_map/reshape | solution.py:374
  5.6 0.0 copy-done.3
  5.6 0.7 %broadcast_in_dim.6.b1_hbm = f32[64,256]{1,0:T(8,128)} broadcast(f32[64]{0:T(128)S(1)} %copy-done.3), dimensions={0} | broadcast | bytes 65792 | tf_op jit(solution)/shard_map/broadcast_in_dim | solution.py:377
  6.3 0.0 copy-done.4
  6.3 0.7 %broadcast_in_dim.7.b2_hbm = f32[64,256]{1,0:T(8,128)} broadcast(f32[64]{0:T(128)S(1)} %copy-done.4), dimensions={0} | broadcast | bytes 65792 | tf_op jit(solution)/shard_map/broadcast_in_dim | solution.py:378
  7.0 49.5 %shard_map.127 = f32[32,512]{1,0:T(8,128)} custom-call(bf16[8,256,512]{2,1,0:T(8,128)(2,1)} %bitcast.25, bf16[8,256,512]{2,1,0:T(8,128)(2,1)} %sens_hbm.1, s32[8,256]{1,0:T(8,128)} %bitcast.29, f32[32,512]{1,0:T(8,128)} %bitcast.28, bf16[2,512,512]{2,1,0:T(8,128)(2,1)} %constant.8.clone.ta_hbm, bf16[2,512,512]{2,1,0:T(8,128)(2,1)} %constant.9.clone.tb_hbm, ...), custom_call_target="tpu_custom_call" | custom-call | tf_op jit(solution)/shard_map/pallas_call | solution.py:382
  56.5 1.5 %copy.36 = f32[1,32,512]{2,1,0:T(8,128)} copy(f32[1,32,512]{2,1,0:T(8,128)} %bitcast.27) | data formatting | bytes 131072
Async XLA Ops:
  0.0 2.6 %copy-start.2 = (bf16[3,8,10,1,1,1]{2,0,5,4,3,1:T(4,128)(2,1)S(1)}, bf16[3,8,10,1,1,1]{2,0,5,4,3,1:T(4,128)(2,1)}, u32[]{:S(2)}) copy-start(bf16[3,8,10,1,1,1]{2,0,5,4,3,1:T(4,128)(2,1)} %constant.16) | copy-start | bytes 1444
  0.0 2.6 %copy-start.1 = (bf16[3,3,3,2,64]{4,3,2,1,0:T(2,128)(2,1)S(1)}, bf16[3,3,3,2,64]{4,3,2,1,0:T(2,128)(2,1)}, u32[]{:S(2)}) copy-start(bf16[3,3,3,2,64]{4,3,2,1,0:T(2,128)(2,1)} %param.21) | copy-start | bytes 20740
  1.3 2.9 %copy-start = (bf16[3,3,3,64,64]{4,3,2,1,0:T(8,128)(2,1)S(1)}, bf16[3,3,3,64,64]{4,3,2,1,0:T(8,128)(2,1)}, u32[]{:S(2)}) copy-start(bf16[3,3,3,64,64]{4,3,2,1,0:T(8,128)(2,1)} %param.19) | copy-start | bytes 663556
  2.6 3.0 %copy-start.3 = (f32[64]{0:T(128)S(1)}, f32[64]{0:T(128)}, u32[]{:S(2)}) copy-start(f32[64]{0:T(128)} %param.18) | copy-start | bytes 772
  2.9 3.4 %copy-start.4 = (f32[64]{0:T(128)S(1)}, f32[64]{0:T(128)}, u32[]{:S(2)}) copy-start(f32[64]{0:T(128)} %param.20) | copy-start | bytes 772

commit v2 on v1

--- a/solution.py
+++ b/solution.py
@@ -52,7 +52,7 @@
     kspace_hbm, sens_hbm, mask_hbm, image_hbm, ta_hbm, tb_hbm, w1_hbm, w2_hbm, w3_hbm, b1_hbm, b2_hbm,
     out_ref,
     ksp, sens, mask, image, ta, tb, w1, w2, w3, b1, b2,
-    xb, ci, cols, acc, gs, grecv, xr, x48, hb, kb, h1, h2, psend, precv,
+    xb, ci, cols, misfit, stacked, acc, gs, grecv, xr, x48, hb, kb, h1, h2, psend, precv,
     lsem, asend, arecv, bsend, brecv, csend, crecv, dsend, drecv,
 ):
     t = lax.axis_index("frame")
@@ -134,32 +134,26 @@
     loads[4].wait()
     loads[5].wait()
 
-    def coil(c):
-        halves = []
+    for c in range(NCO):
         for half in range(2):
             est = dot(tb[0, half * ROWS : (half + 1) * ROWS, :], cols[c])
             k = ksp[c, :, half * N : (half + 1) * N].astype(F32)
-            halves.append((est - k).astype(BF16))
-        misfit = jnp.concatenate(halves, axis=1)
-        stacked = jnp.concatenate(
-            [dot(misfit, ta[1, :, half * N : (half + 1) * N]).astype(BF16) for half in range(2)], axis=0
-        )
-        m = mask[pl.ds(c, 1), :].astype(F32).astype(BF16)
+            misfit[c, :, half * N : (half + 1) * N] = (est - k).astype(BF16)
+    for c in range(NCO):
+        for half in range(2):
+            stacked[c, half * ROWS : (half + 1) * ROWS, :] = dot(
+                misfit[c], ta[1, :, half * N : (half + 1) * N]
+            ).astype(BF16)
+    for c in range(NCO):
+        m = mask[c : c + 1, :].astype(F32).astype(BF16)
         mm = jnp.concatenate([m, m], axis=1)
-        b_re = dot(tb[1, :ROWS, :] * mm, stacked)
-        b_im = dot(tb[1, ROWS:, :] * mm, stacked)
+        b_re = dot(tb[1, :ROWS, :] * mm, stacked[c])
+        b_im = dot(tb[1, ROWS:, :] * mm, stacked[c])
         s_re, s_im = sens[c, :, :N].astype(F32), sens[c, :, N:].astype(F32)
-        return s_re * b_re + s_im * b_im, s_re * b_im - s_im * b_re
-
-    first_re, first_im = coil(0)
-    acc[:, :N] = first_re
-    acc[:, N:] = first_im
-
-    @pl.loop(1, NCO)
-    def _(c):
-        g_re, g_im = coil(c)
-        acc[:, :N] += g_re
-        acc[:, N:] += g_im
+        g_re = s_re * b_re + s_im * b_im
+        g_im = s_re * b_im - s_im * b_re
+        acc[:, :N] = g_re if c == 0 else acc[:, :N] + g_re
+        acc[:, N:] = g_im if c == 0 else acc[:, N:] + g_im
 
     gs[:ROWS, :] = pltpu.roll(acc[...], 3, axis=0).astype(BF16)
     gs[ROWS : ROWS + 16, :] = pltpu.roll(acc[ROWS - 16 :, :], 3, axis=0).astype(BF16)
@@ -241,13 +235,12 @@
 
     bias1 = b1[...]
     for f in range(3):
-        @pl.loop(0, 5)
-        def _(i):
+        for i in range(5):
             here_k = kb[i, f * HR : (f + 3) * HR, :]
             next_k = kb[i + 1, f * HR : (f + 3) * HR, :]
             top = dot(w1[:384, :], here_k)
             low = dot(w1[384:512, :], here_k) + dot(w1[512:, :], next_k)
-            base = pl.multiple_of(i * 512, 512)
+            base = i * 512
             for q in range(6):
                 h1[f, pl.ds(base + q * CH, CH), :] = jnp.maximum(top[q * CH : (q + 1) * CH] + bias1, 0.0).astype(BF16)
             for q in range(2):
@@ -271,15 +264,13 @@
 
     bias2 = b2[...]
 
-    @pl.loop(0, 17)
-    def _(i):
-        for q in range(2):
-            base = pl.multiple_of((2 * i + q) * CH, CH)
-            taps = dot(w2[0], h1[0, pl.ds(base, 3 * CH), :])
-            taps += dot(w2[1], h1[1, pl.ds(base, 3 * CH), :])
-            taps += dot(w2[2], h1[2, pl.ds(base, 3 * CH), :])
-            v = taps[CH : 2 * CH] + shift_right(taps[:CH]) + shift_left(taps[2 * CH :]) + bias2
-            h2[pl.ds(base, CH), :] = jnp.maximum(v, 0.0).astype(BF16)
+    for r in range(34):
+        base = r * CH
+        taps = dot(w2[0], h1[0, base : base + 3 * CH, :])
+        taps += dot(w2[1], h1[1, base : base + 3 * CH, :])
+        taps += dot(w2[2], h1[2, base : base + 3 * CH, :])
+        v = taps[CH : 2 * CH] + shift_right(taps[:CH]) + shift_left(taps[2 * CH :]) + bias2
+        h2[base : base + CH, :] = jnp.maximum(v, 0.0).astype(BF16)
 
     @pl.when(j == 0)
     def _():
@@ -289,12 +280,11 @@
     def _():
         h2[33 * CH :, :] = jnp.zeros((CH, N), BF16)
 
-    @pl.loop(0, RB // 8)
-    def _(i):
-        base = pl.multiple_of(i * 8 * CH, 8 * CH)
-        taps = dot(w3[...], h2[pl.ds(base, 10 * CH), :])
+    for i in range(RB // 8):
+        base = i * 8 * CH
+        taps = dot(w3[...], h2[base : base + 10 * CH, :])
         v = taps[48:96] + shift_right(taps[:48]) + shift_left(taps[96:])
-        ri = pl.multiple_of(i * 8, 8)
+        ri = i * 8
         for a in range(3):
             for half in range(2):
                 o = (a * 2 + half) * 8
@@ -389,6 +379,8 @@
             pltpu.VMEM((ROWS, 2 * N), BF16),
             pltpu.VMEM((NCO * RB, 2 * N), BF16),
             pltpu.VMEM((NCO, 2 * ROWS, N), BF16),
+            pltpu.VMEM((NCO, ROWS, 2 * N), BF16),
+            pltpu.VMEM((NCO, 2 * ROWS, N), BF16),
             pltpu.VMEM((ROWS, 2 * N), F32),
             pltpu.VMEM((ROWS + 16, 2 * N), BF16),
             pltpu.VMEM((GRP, HR, 2 * N), BF16),

time: 58.2 us -> 48.3 us (0.83)
  Pallas kernels: 49.5 us -> 39.6 us
    pallas_call x1, Pallas kernels: 49.5 us -> 39.6 us  [shards(): pl.pallas_call(functools.partial(kernel, frames), out_shape=jax.ShapeDtyp...]
where the time goes in v2:
time: 48.3 us; the launch traced here: 48.1 us
  Pallas kernels  39.6 us (82%)
  local copies, waits for them, and re-layouts  6.93 us (14%)
  matrix products  1.48 us (3%)
    pallas_call x1, Pallas kernels, shards(): pl.pallas_call(functools.partial(kernel, frames), out_shape=jax.ShapeDtyp...  39.6 us
    unnamed x11, local copies, waits for them, and re-layouts  1.5 us
    reshape x2, local copies, waits for them, and re-layouts, shards(): jnp.einsum('abeoc,bqu->qoaceu', w_first, pick1).reshape(10 * CH, 3 * HR)  1.25 us
    dot_general x1, matrix products, shards(): jnp.einsum('abeoc,bqu->qoaceu', w_first, pick1).reshape(10 * CH, 3 * HR)  1.12 us
    reshape x1, local copies, waits for them, and re-layouts, shards(): w2 = jnp.transpose(w_mid, (0, 2, 3, 1, 4)).reshape(3, 3 * CH, 3 * CH)  1.07 us
    reshape x1, local copies, waits for them, and re-layouts, shards(): w3 = jnp.einsum('abeoi,bqu->eaoqui', w_last, pick3).reshape(144, 10 * CH)  1.04 us

profile of v2, /device:TPU:30, one launch (start us, length us, event | category | flops | bytes accessed | tf_op | source)
XLA Modules:
  0.0 48.1 jit_solution(11441002439110876153)
XLA Ops:
  0.0 0.0 copy-start.2
  0.0 0.0 copy-start.1
  0.0 1.1 %convolution_bitcast_fusion.1 = bf16[10,64,3,2,3,8]{1,0,3,4,2,5:T(8,128)(2,1)S(1)} fusion(bf16[3,10,8,1,1,1]{1,0,5,4,3,2:T(4,128)(2,1)} %constant.15, bf16[3,3,3,64,2]{3,4,2,1,0:T(2,128)(2,1)} %param.17), kind=kOutput, calls=%fused_computation.1 | convolution fusion | flops 552960 | bytes 191712 | tf_op jit(solution)/shard_map/abeoc,bqu->qoaceu/dot_general | solution.py:363
  1.1 0.2 copy.20
  1.3 0.0 copy-start
  1.3 0.4 reshape.11
  1.7 0.9 %copy.24.w1_hbm = bf16[640,144]{1,0:T(8,128)(2,1)} copy(bf16[640,144]{0,1:T(8,128)(2,1)S(1)} %reshape.11) | data formatting | bytes 368640 | tf_op jit(solution)/shard_map/reshape | solution.py:363
  2.6 0.0 copy-done.2
  2.6 0.0 copy-done.1
  2.6 0.0 copy-start.3
  2.6 0.4 convolution_bitcast_fusion
  2.9 0.0 copy-start.4
  3.0 0.2 copy.23
  3.1 1.0 %reshape.13.w3_hbm = bf16[144,640]{1,0:T(8,128)(2,1)} reshape(bf16[3,3,2,8,10,64]{5,4,3,2,1,0:T(8,128)(2,1)S(1)} %copy.23) | data formatting | bytes 368640 | tf_op jit(solution)/shard_map/reshape | solution.py:366
  4.1 0.0 copy-done
  4.1 0.4 copy.21
  4.5 1.1 %reshape.12.w2_hbm = bf16[3,192,192]{2,1,0:T(8,128)(2,1)} reshape(bf16[3,3,64,3,64]{4,3,2,1,0:T(4,128)(2,1)S(1)} %copy.21) | data formatting | bytes 442368 | tf_op jit(solution)/shard_map/reshape | solution.py:364
  5.6 0.0 copy-done.3
  5.6 0.7 %broadcast_in_dim.6.b1_hbm = f32[64,256]{1,0:T(8,128)} broadcast(f32[64]{0:T(128)S(1)} %copy-done.3), dimensions={0} | broadcast | bytes 65792 | tf_op jit(solution)/shard_map/broadcast_in_dim | solution.py:367
  6.3 0.0 copy-done.4
  6.3 0.7 %broadcast_in_dim.7.b2_hbm = f32[64,256]{1,0:T(8,128)} broadcast(f32[64]{0:T(128)S(1)} %copy-done.4), dimensions={0} | broadcast | bytes 65792 | tf_op jit(solution)/shard_map/broadcast_in_dim | solution.py:368
  7.0 39.6 %shard_map.127 = f32[32,512]{1,0:T(8,128)} custom-call(bf16[8,256,512]{2,1,0:T(8,128)(2,1)} %bitcast.25, bf16[8,256,512]{2,1,0:T(8,128)(2,1)} %sens_hbm.1, s32[8,256]{1,0:T(8,128)} %bitcast.29, f32[32,512]{1,0:T(8,128)} %bitcast.28, bf16[2,512,512]{2,1,0:T(8,128)(2,1)} %constant.8.clone.ta_hbm, bf16[2,512,512]{2,1,0:T(8,128)(2,1)} %constant.9.clone.tb_hbm, ...), custom_call_target="tpu_custom_call" | custom-call | tf_op jit(solution)/shard_map/pallas_call | solution.py:372
  46.7 1.5 %copy.36 = f32[1,32,512]{2,1,0:T(8,128)} copy(f32[1,32,512]{2,1,0:T(8,128)} %bitcast.27) | data formatting | bytes 131072
Async XLA Ops:
  0.0 2.6 %copy-start.2 = (bf16[3,8,10,1,1,1]{2,0,5,4,3,1:T(4,128)(2,1)S(1)}, bf16[3,8,10,1,1,1]{2,0,5,4,3,1:T(4,128)(2,1)}, u32[]{:S(2)}) copy-start(bf16[3,8,10,1,1,1]{2,0,5,4,3,1:T(4,128)(2,1)} %constant.16) | copy-start | bytes 1444
  0.0 2.6 %copy-start.1 = (bf16[3,3,3,2,64]{4,3,2,1,0:T(2,128)(2,1)S(1)}, bf16[3,3,3,2,64]{4,3,2,1,0:T(2,128)(2,1)}, u32[]{:S(2)}) copy-start(bf16[3,3,3,2,64]{4,3,2,1,0:T(2,128)(2,1)} %param.21) | copy-start | bytes 20740
  1.3 2.9 %copy-start = (bf16[3,3,3,64,64]{4,3,2,1,0:T(8,128)(2,1)S(1)}, bf16[3,3,3,64,64]{4,3,2,1,0:T(8,128)(2,1)}, u32[]{:S(2)}) copy-start(bf16[3,3,3,64,64]{4,3,2,1,0:T(8,128)(2,1)} %param.19) | copy-start | bytes 663556
  2.6 3.0 %copy-start.3 = (f32[64]{0:T(128)S(1)}, f32[64]{0:T(128)}, u32[]{:S(2)}) copy-start(f32[64]{0:T(128)} %param.18) | copy-start | bytes 772
  2.9 3.4 %copy-start.4 = (f32[64]{0:T(128)S(1)}, f32[64]{0:T(128)}, u32[]{:S(2)}) copy-start(f32[64]{0:T(128)} %param.20) | copy-start | bytes 772

commit v3 on v2

--- a/solution.py
+++ b/solution.py
@@ -26,11 +26,7 @@
     ang = (idx[:, None] * idx[None, :] % N) * (2.0 * np.pi / N)
     fr = (np.cos(ang) / np.sqrt(N)).astype(np.float32)
     fi = (-np.sin(ang) / np.sqrt(N)).astype(np.float32)
-    cols = np.block([[fr, fi], [-fi, fr]])
-    back = np.block([[fr, -fi], [fi, fr]])
-    rows = np.block([[fr, -fi], [fi, fr]])
-    rback = np.block([[fr, fi], [-fi, fr]])
-    return cols, back, rows, rback
+    return np.stack([np.block([[fr, fi], [-fi, fr]]), np.block([[fr, -fi], [fi, fr]])])
 
 
 def shift_right(v):
@@ -47,11 +43,52 @@
     return jnp.dot(a, b, preferred_element_type=F32)
 
 
+def iota2(shape):
+    return lax.broadcasted_iota(jnp.int32, shape, 0), lax.broadcasted_iota(jnp.int32, shape, 1)
+
+
+def conv_weights(pick, wf, wm, wl, bf, bm, w54, w1, w2, w3):
+    w54[...] = jnp.zeros((64, CH), F32)
+    for k in range(27):
+        w54[2 * k : 2 * k + 2, :] = wf[k].astype(F32)
+    source = w54[...].astype(BF16)
+    row, col = iota2((640, CH))
+    tile = ((row & (CH - 1)) == col).astype(F32).astype(BF16)
+    row, col = iota2((640, 144))
+    base = jnp.where(row >= 512, (row >> 6) - 10, row >> 6)
+    total = jnp.zeros((640, 144), F32)
+    for b in range(3):
+        z = dot(pick[b], source).astype(BF16)
+        part = lax.dot_general(tile, z, (((1,), (1,)), ((), ())), preferred_element_type=F32)
+        total = jnp.where((col & 7) == base + b, part, total)
+    w1[...] = total.astype(BF16)
+    for k in range(27):
+        w54[2 * k : 2 * k + 2, :] = wl[k].astype(F32)
+    source = w54[...].astype(BF16)
+    row, col = iota2((CH, 640))
+    tile = (row == (col & (CH - 1))).astype(F32).astype(BF16)
+    row, col = iota2((144, 640))
+    total = jnp.zeros((144, 640), F32)
+    for b in range(3):
+        z = dot(pick[3 + b], source).astype(BF16)
+        total = jnp.where((col >> 6) == (row & 7) + b, dot(z, tile), total)
+    w3[...] = total.astype(BF16)
+    row, col = iota2((CH, 3 * CH))
+    places = [(col == row + b * CH).astype(F32).astype(BF16) for b in range(3)]
+    for a in range(3):
+        for e in range(3):
+            w2[a, e * CH : (e + 1) * CH, :] = sum(
+                dot(wm[(a * 3 + b) * 3 + e], places[b]) for b in range(3)
+            ).astype(BF16)
+    return [jnp.broadcast_to(v[...], (N, CH)).T for v in (bf, bm)]
+
+
 def kernel(
     frames,
-    kspace_hbm, sens_hbm, mask_hbm, image_hbm, ta_hbm, tb_hbm, w1_hbm, w2_hbm, w3_hbm, b1_hbm, b2_hbm,
+    kspace_hbm, sens_hbm, mask_hbm, image_hbm, table_hbm, pick_hbm, wf_hbm, wm_hbm, wl_hbm, bf_hbm, bm_hbm,
     out_ref,
-    ksp, sens, mask, image, ta, tb, w1, w2, w3, b1, b2,
+    ksp, sens, mask, image, table, pick, wf, wm, wl, bf, bm,
+    w54, w1, w2, w3,
     xb, ci, cols, misfit, stacked, acc, gs, grecv, xr, x48, hb, kb, h1, h2, psend, precv,
     lsem, asend, arecv, bsend, brecv, csend, crecv, dsend, drecv,
 ):
@@ -63,8 +100,8 @@
         pltpu.make_async_copy(src, dst, lsem.at[i])
         for i, (src, dst) in enumerate(
             [
-                (image_hbm, image), (sens_hbm, sens), (ta_hbm, ta), (tb_hbm, tb), (kspace_hbm, ksp),
-                (mask_hbm, mask), (w1_hbm, w1), (w2_hbm, w2), (w3_hbm, w3), (b1_hbm, b1), (b2_hbm, b2),
+                (image_hbm, image), (pick_hbm, pick), (wf_hbm, wf), (wm_hbm, wm), (wl_hbm, wl), (bf_hbm, bf),
+                (bm_hbm, bm), (sens_hbm, sens), (table_hbm, table), (kspace_hbm, ksp), (mask_hbm, mask),
             ]
         )
     ]
@@ -83,6 +120,9 @@
 
     loads[0].wait()
     xb[pl.ds(r0, RB), :] = image[...].astype(BF16)
+    for c in loads[1:7]:
+        c.wait()
+    bias1, bias2 = conv_weights(pick, wf, wm, wl, bf, bm, w54, w1, w2, w3)
     present = sum(here.astype(jnp.int32) for _, here in partners)
     pl.semaphore_wait(barrier, GRP - 1 + present)
 
@@ -99,8 +139,8 @@
         c.start()
         acopy.append(c)
 
-    loads[1].wait()
-    loads[2].wait()
+    loads[7].wait()
+    loads[8].wait()
 
     def columns(q):
         rq = pl.multiple_of(q * RB, RB)
@@ -112,7 +152,7 @@
             ci[c * RB : (c + 1) * RB, :N] = (s_re * x_re - s_im * x_im).astype(BF16)
             ci[c * RB : (c + 1) * RB, N:] = (s_re * x_im + s_im * x_re).astype(BF16)
         for half in range(2):
-            spec = dot(ci[...], ta[0, :, half * N : (half + 1) * N]).astype(BF16)
+            spec = dot(ci[...], table[0, :, half * N : (half + 1) * N]).astype(BF16)
             for c in range(NCO):
                 cols[c, pl.ds(half * ROWS + rq, RB), :] = spec[c * RB : (c + 1) * RB]
 
@@ -130,25 +170,24 @@
         ).wait_recv()
         columns(lax.rem(j - s + GRP, GRP))
 
-    loads[3].wait()
-    loads[4].wait()
-    loads[5].wait()
+    loads[9].wait()
+    loads[10].wait()
 
     for c in range(NCO):
         for half in range(2):
-            est = dot(tb[0, half * ROWS : (half + 1) * ROWS, :], cols[c])
+            est = dot(table[1, half * ROWS : (half + 1) * ROWS, :], cols[c])
             k = ksp[c, :, half * N : (half + 1) * N].astype(F32)
             misfit[c, :, half * N : (half + 1) * N] = (est - k).astype(BF16)
     for c in range(NCO):
         for half in range(2):
             stacked[c, half * ROWS : (half + 1) * ROWS, :] = dot(
-                misfit[c], ta[1, :, half * N : (half + 1) * N]
+                misfit[c], table[1, :, half * N : (half + 1) * N]
             ).astype(BF16)
     for c in range(NCO):
         m = mask[c : c + 1, :].astype(F32).astype(BF16)
         mm = jnp.concatenate([m, m], axis=1)
-        b_re = dot(tb[1, :ROWS, :] * mm, stacked[c])
-        b_im = dot(tb[1, ROWS:, :] * mm, stacked[c])
+        b_re = dot(table[0, :ROWS, :] * mm, stacked[c])
+        b_im = dot(table[0, ROWS:, :] * mm, stacked[c])
         s_re, s_im = sens[c, :, :N].astype(F32), sens[c, :, N:].astype(F32)
         g_re = s_re * b_re + s_im * b_im
         g_im = s_re * b_im - s_im * b_re
@@ -176,8 +215,6 @@
     xr[ROWS : ROWS + 16, :] = jnp.zeros((16, 2 * N), F32)
     x48[...] = xr[pl.ds(r0, HR), :]
     x48[3 : 3 + RB, :] = image[...]
-    for c in loads[6:]:
-        c.wait()
     total = x48[...] - gs[pl.ds(r0, HR), :].astype(F32)
     for c in bcopy:
         c.wait_recv()
@@ -233,7 +270,6 @@
 
         planes(2 + d)
 
-    bias1 = b1[...]
     for f in range(3):
         for i in range(5):
             here_k = kb[i, f * HR : (f + 3) * HR, :]
@@ -262,8 +298,6 @@
     def _():
         h1[2] = jnp.zeros((40 * CH, N), BF16)
 
-    bias2 = b2[...]
-
     for r in range(34):
         base = r * CH
         taps = dot(w2[0], h1[0, base : base + 3 * CH, :])
@@ -343,39 +377,35 @@
             ).wait_send()
 
 
-def spread(rows, width, first):
-    out = np.zeros((3, rows, width), np.float32)
-    for q in range(rows):
-        for b in range(3):
-            u = q + first + b
-            if 0 <= u < width:
-                out[b, q, u] = 1
+def picks():
+    out = np.zeros((6, 144, 64), np.float32)
+    for b in range(3):
+        for k in range(18):
+            a, ch, e = k // 6, k // 3 % 2, k % 3
+            out[b, 8 * k : 8 * k + 8, ((a * 3 + b) * 3 + e) * 2 + ch] = 1
+            e, a, ch = k // 6, k // 2 % 3, k % 2
+            out[3 + b, 8 * k : 8 * k + 8, ((a * 3 + b) * 3 + e) * 2 + ch] = 1
     return out
 
 
 def shards(frames, kspace, sens, mask, image, w_first, b_first, w_mid, b_mid, w_last):
-    cols, back, rows, rback = dft_tables()
-    ta = jnp.asarray(np.stack([cols, back]), BF16)
-    tb = jnp.asarray(np.stack([rows, rback]), BF16)
-    here = spread(8, 8, 0)
-    ahead = spread(2, 8, -2)
-    pick1 = jnp.asarray(np.concatenate([here, ahead], axis=1), BF16)
-    w1 = jnp.einsum("abeoc,bqu->qoaceu", w_first, pick1).reshape(10 * CH, 3 * HR)
-    w2 = jnp.transpose(w_mid, (0, 2, 3, 1, 4)).reshape(3, 3 * CH, 3 * CH)
-    pick3 = jnp.asarray(spread(8, 10, 0), BF16)
-    w3 = jnp.einsum("abeoi,bqu->eaoqui", w_last, pick3).reshape(144, 10 * CH)
-    b1 = jnp.broadcast_to(b_first[:, None], (CH, N))
-    b2 = jnp.broadcast_to(b_mid[:, None], (CH, N))
-    args = (kspace[0], sens, mask[0], image[0], ta, tb, w1, w2, w3, b1, b2)
-    order = args
+    args = (
+        kspace[0], sens, mask[0], image[0], jnp.asarray(dft_tables(), BF16), jnp.asarray(picks(), BF16),
+        jnp.swapaxes(w_first, 3, 4).reshape(27, 2, CH), w_mid.reshape(27, CH, CH), w_last.reshape(27, 2, CH),
+        b_first[None], b_mid[None],
+    )
     dma = pltpu.SemaphoreType.DMA
     out = pl.pallas_call(
         functools.partial(kernel, frames),
         out_shape=jax.ShapeDtypeStruct((RB, 2 * N), F32),
         in_specs=[pl.BlockSpec(memory_space=pl.ANY)] * len(args),
         out_specs=pl.BlockSpec(memory_space=pltpu.VMEM),
-        scratch_shapes=[pltpu.VMEM(a.shape, a.dtype) for a in order]
+        scratch_shapes=[pltpu.VMEM(a.shape, a.dtype) for a in args]
         + [
+            pltpu.VMEM((64, CH), F32),
+            pltpu.VMEM((640, 144), BF16),
+            pltpu.VMEM((3, 3 * CH, 3 * CH), BF16),
+            pltpu.VMEM((144, 640), BF16),
             pltpu.VMEM((ROWS, 2 * N), BF16),
             pltpu.VMEM((NCO * RB, 2 * N), BF16),
             pltpu.VMEM((NCO, 2 * ROWS, N), BF16),

time: 48.3 us -> 41.6 us (0.86)
  the two profiles are of different devices: /device:TPU:30 before, /device:TPU:28 now
where the time goes in v3:
time: 41.6 us; the launch traced here: 41.5 us
  Pallas kernels  40 us (96%)
  local copies, waits for them, and re-layouts  1.47 us (4%)
    pallas_call x1, Pallas kernels, shards(): pl.pallas_call(functools.partial(kernel, frames), out_shape=jax.ShapeDtyp...  40 us
    unnamed x1, local copies, waits for them, and re-layouts  1.47 us

profile of v3, /device:TPU:28, one launch (start us, length us, event | category | flops | bytes accessed | tf_op | source)
XLA Modules:
  0.0 41.5 jit_solution(2086374929659620245)
XLA Ops:
  0.0 40.0 %shard_map.109 = f32[32,512]{1,0:T(8,128)} custom-call(bf16[8,256,512]{2,1,0:T(8,128)(2,1)} %bitcast.11, bf16[8,256,512]{2,1,0:T(8,128)(2,1)} %sens_hbm.1, s32[8,256]{1,0:T(8,128)} %bitcast.17, f32[32,512]{1,0:T(8,128)} %bitcast.14, bf16[2,512,512]{2,1,0:T(8,128)(2,1)} %constant.4.clone.table_hbm, bf16[6,144,64]{2,1,0:T(8,128)(2,1)} %constant.5.clone.pick_hbm, ...), custom_call_target="tpu_custom_call" | custom-call | tf_op jit(solution)/shard_map/pallas_call | solution.py:398
  40.0 1.5 %copy.13 = f32[1,32,512]{2,1,0:T(8,128)} copy(f32[1,32,512]{2,1,0:T(8,128)} %bitcast.13) | data formatting | bytes 131072

commit v4 on v3

--- a/solution.py
+++ b/solution.py
@@ -15,7 +15,8 @@
 ROWS = 256
 N = 256
 RB = 32
-HR = 48
+HR = 40
+KF = 48
 NCO = 8
 CH = 64
 GRP = 8
@@ -89,7 +90,7 @@
     out_ref,
     ksp, sens, mask, image, table, pick, wf, wm, wl, bf, bm,
     w54, w1, w2, w3,
-    xb, ci, cols, misfit, stacked, acc, gs, grecv, xr, x48, hb, kb, h1, h2, psend, precv,
+    xb, ci, cols, misfit, stacked, acc, gs, grecv, xr, xh, hb, kb, h1, h2, psend, precv,
     lsem, asend, arecv, bsend, brecv, csend, crecv, dsend, drecv,
 ):
     t = lax.axis_index("frame")
@@ -108,7 +109,7 @@
     for c in loads:
         c.start()
 
-    partners = [(d, (t + d >= 0) & (t + d < frames)) for d in (-2, -1, 1, 2)]
+    partners = [(d, (t + d >= 0) & (t + d < frames)) for d in (-2, 2, -1, 1)]
 
     barrier = pltpu.get_barrier_semaphore()
     for s in range(1, GRP):
@@ -194,14 +195,17 @@
         acc[:, :N] = g_re if c == 0 else acc[:, :N] + g_re
         acc[:, N:] = g_im if c == 0 else acc[:, N:] + g_im
 
-    gs[:ROWS, :] = pltpu.roll(acc[...], 3, axis=0).astype(BF16)
-    gs[ROWS : ROWS + 16, :] = pltpu.roll(acc[ROWS - 16 :, :], 3, axis=0).astype(BF16)
+    xr[:ROWS, :] = pltpu.roll(acc[...], 3, axis=0)
+    xr[ROWS:, :] = pltpu.roll(acc[ROWS - 16 :, :], 3, axis=0)
+    for q in range(GRP):
+        rows = slice(q * RB, q * RB + HR)
+        gs[q] = jnp.concatenate([xr[rows, :N], xr[rows, N:]], axis=0).astype(BF16)
 
     bcopy = []
     for s in range(1, GRP):
         to = lax.rem(j + s, GRP)
         c = pltpu.make_async_remote_copy(
-            src_ref=gs.at[pl.ds(pl.multiple_of(to * RB, RB), HR)],
+            src_ref=gs.at[to],
             dst_ref=grecv.at[s],
             send_sem=bsend.at[s],
             recv_sem=brecv.at[s],
@@ -212,17 +216,20 @@
         bcopy.append(c)
 
     xr[:ROWS, :] = pltpu.roll(xb[...].astype(F32), 3, axis=0)
-    xr[ROWS : ROWS + 16, :] = jnp.zeros((16, 2 * N), F32)
-    x48[...] = xr[pl.ds(r0, HR), :]
-    x48[3 : 3 + RB, :] = image[...]
-    total = x48[...] - gs[pl.ds(r0, HR), :].astype(F32)
+    xr[ROWS:, :] = jnp.zeros((16, 2 * N), F32)
+    for half in range(2):
+        cut = slice(half * N, (half + 1) * N)
+        xh[half * HR : (half + 1) * HR, :] = xr[pl.ds(r0, HR), cut]
+        xh[half * HR + 3 : half * HR + 3 + RB, :] = image[:, cut]
+    total = xh[...] - gs[j].astype(F32)
     for c in bcopy:
         c.wait_recv()
     for s in range(1, GRP):
         total = total - grecv[s].astype(F32)
-    row = r0 - 3 + lax.broadcasted_iota(jnp.int32, (HR, 2 * N), 0)
+    line = lax.broadcasted_iota(jnp.int32, (2 * HR, N), 0)
+    row = r0 - 3 + jnp.where(line >= HR, line - HR, line)
     total = jnp.where((row >= 0) & (row < ROWS), total, 0.0)
-    x48[...] = total
+    xh[...] = total
     hb[2] = total.astype(BF16)
 
     for d, here in partners:
@@ -242,22 +249,21 @@
 
         @pl.when(jnp.logical_not(here))
         def _():
-            hb[2 + d] = jnp.zeros((HR, 2 * N), BF16)
+            hb[2 + d] = jnp.zeros((2 * HR, N), BF16)
 
     def planes(f):
         v = hb[f].astype(F32)
         parts = []
         for half in range(2):
-            p = v[:, half * N : (half + 1) * N]
+            p = v[half * HR : (half + 1) * HR]
             parts += [shift_right(p), p, shift_left(p)]
         for i in range(HR // 8):
-            kb[i, f * HR : (f + 1) * HR, :] = jnp.concatenate(
+            kb[i, f * KF : (f + 1) * KF, :] = jnp.concatenate(
                 [p[8 * i : 8 * i + 8] for p in parts], axis=0
             ).astype(BF16)
 
-    planes(2)
-    for d, here in partners:
-        @pl.when(here)
+    def arrived(d):
+        @pl.when((t + d >= 0) & (t + d < frames))
         def _():
             pltpu.make_async_remote_copy(
                 src_ref=hb.at[2],
@@ -270,17 +276,33 @@
 
         planes(2 + d)
 
-    for f in range(3):
+    def first(f):
+        def put(q, v):
+            h1[f, q * CH : (q + 1) * CH, :] = jnp.maximum(v + bias1, 0.0).astype(BF16)
+
         for i in range(5):
-            here_k = kb[i, f * HR : (f + 3) * HR, :]
-            next_k = kb[i + 1, f * HR : (f + 3) * HR, :]
-            top = dot(w1[:384, :], here_k)
-            low = dot(w1[384:512, :], here_k) + dot(w1[512:, :], next_k)
-            base = i * 512
+            here_k = kb[i, f * KF : (f + 3) * KF, :]
+            if i == 4:
+                top = dot(w1[: 4 * CH, :], here_k)
+                for q in range(4):
+                    put(32 + q, top[q * CH : (q + 1) * CH])
+                continue
+            next_k = kb[i + 1, f * KF : (f + 3) * KF, :]
+            top = dot(w1[: 6 * CH, :], here_k)
+            low = dot(w1[6 * CH : 8 * CH, :], here_k) + dot(w1[8 * CH :, :], next_k)
             for q in range(6):
-                h1[f, pl.ds(base + q * CH, CH), :] = jnp.maximum(top[q * CH : (q + 1) * CH] + bias1, 0.0).astype(BF16)
+                put(8 * i + q, top[q * CH : (q + 1) * CH])
             for q in range(2):
-                h1[f, pl.ds(base + (6 + q) * CH, CH), :] = jnp.maximum(low[q * CH : (q + 1) * CH] + bias1, 0.0).astype(BF16)
+                put(8 * i + 6 + q, low[q * CH : (q + 1) * CH])
+
+    planes(2)
+    arrived(-1)
+    arrived(1)
+    first(1)
+    arrived(-2)
+    first(0)
+    arrived(2)
+    first(2)
 
     @pl.when(j == 0)
     def _():
@@ -288,15 +310,15 @@
 
     @pl.when(j == GRP - 1)
     def _():
-        h1[:, 34 * CH :, :] = jnp.zeros((3, 6 * CH, N), BF16)
+        h1[:, 34 * CH :, :] = jnp.zeros((3, 2 * CH, N), BF16)
 
     @pl.when(t == 0)
     def _():
-        h1[0] = jnp.zeros((40 * CH, N), BF16)
+        h1[0] = jnp.zeros((36 * CH, N), BF16)
 
     @pl.when(t == frames - 1)
     def _():
-        h1[2] = jnp.zeros((40 * CH, N), BF16)
+        h1[2] = jnp.zeros((36 * CH, N), BF16)
 
     for r in range(34):
         base = r * CH
@@ -314,17 +336,22 @@
     def _():
         h2[33 * CH :, :] = jnp.zeros((CH, N), BF16)
 
+    blocks = []
     for i in range(RB // 8):
         base = i * 8 * CH
         taps = dot(w3[...], h2[base : base + 10 * CH, :])
-        v = taps[48:96] + shift_right(taps[:48]) + shift_left(taps[96:])
-        ri = i * 8
-        for a in range(3):
-            for half in range(2):
-                o = (a * 2 + half) * 8
-                psend[a, pl.ds(ri, 8), half * N : (half + 1) * N] = v[o : o + 8]
-
-    ends = [(1, 0, t + 1 < frames), (-1, 2, t >= 1)]
+        blocks.append(taps[48:96] + shift_right(taps[:48]) + shift_left(taps[96:]))
+    for a in (0, 2, 1):
+        for half in range(2):
+            o = (a * 2 + half) * 8
+            v = jnp.concatenate([b[o : o + 8] for b in blocks], axis=0)
+            cut = slice(half * N, (half + 1) * N)
+            if a == 1:
+                xh[half * HR + 3 : half * HR + 3 + RB, :] += v
+            else:
+                psend[a // 2, :, cut] = v.astype(BF16)
+
+    ends = [(1, 0, t + 1 < frames), (-1, 1, t >= 1)]
     for n, (d, a, here) in enumerate(ends):
         @pl.when(here)
         def _():
@@ -337,7 +364,8 @@
                 device_id_type=MESH,
             ).start()
 
-    out_ref[...] = x48[3 : 3 + RB, :] + psend[1]
+    for half in range(2):
+        out_ref[:, half * N : (half + 1) * N] = xh[half * HR + 3 : half * HR + 3 + RB, :]
     for n, (d, a, here) in enumerate(ends):
         @pl.when((t - d >= 0) & (t - d < frames))
         def _():
@@ -349,7 +377,7 @@
                 device_id={"frame": t - d},
                 device_id_type=MESH,
             ).wait_recv()
-            out_ref[...] += precv[n]
+            out_ref[...] += precv[n].astype(F32)
 
     for c in acopy + bcopy:
         c.wait_send()
@@ -397,7 +425,7 @@
     dma = pltpu.SemaphoreType.DMA
     out = pl.pallas_call(
         functools.partial(kernel, frames),
-        out_shape=jax.ShapeDtypeStruct((RB, 2 * N), F32),
+        out_shape=pltpu.VMEM((RB, 2 * N), F32),
         in_specs=[pl.BlockSpec(memory_space=pl.ANY)] * len(args),
         out_specs=pl.BlockSpec(memory_space=pltpu.VMEM),
         scratch_shapes=[pltpu.VMEM(a.shape, a.dtype) for a in args]
@@ -412,16 +440,16 @@
             pltpu.VMEM((NCO, ROWS, 2 * N), BF16),
             pltpu.VMEM((NCO, 2 * ROWS, N), BF16),
             pltpu.VMEM((ROWS, 2 * N), F32),
-            pltpu.VMEM((ROWS + 16, 2 * N), BF16),
-            pltpu.VMEM((GRP, HR, 2 * N), BF16),
+            pltpu.VMEM((GRP, 2 * HR, N), BF16),
+            pltpu.VMEM((GRP, 2 * HR, N), BF16),
             pltpu.VMEM((ROWS + 16, 2 * N), F32),
-            pltpu.VMEM((HR, 2 * N), F32),
-            pltpu.VMEM((5, HR, 2 * N), BF16),
-            pltpu.VMEM((HR // 8, 5 * HR, N), BF16),
-            pltpu.VMEM((3, 40 * CH, N), BF16),
+            pltpu.VMEM((2 * HR, N), F32),
+            pltpu.VMEM((5, 2 * HR, N), BF16),
+            pltpu.VMEM((HR // 8, 5 * KF, N), BF16),
+            pltpu.VMEM((3, 36 * CH, N), BF16),
             pltpu.VMEM((34 * CH, N), BF16),
-            pltpu.VMEM((3, RB, 2 * N), F32),
-            pltpu.VMEM((2, RB, 2 * N), F32),
+            pltpu.VMEM((2, RB, 2 * N), BF16),
+            pltpu.VMEM((2, RB, 2 * N), BF16),
             dma((len(args),)), dma((GRP,)), dma((GRP,)), dma((GRP,)), dma((GRP,)),
             dma((5,)), dma((5,)), dma((2,)), dma((2,)),
         ],

time: 41.6 us -> 39.1 us (0.940)
  the two profiles are of different devices: /device:TPU:28 before, /device:TPU:30 now
where the time goes in v4:
time: 39.1 us; the launch traced here: 38.6 us
  Pallas kernels  37.9 us (97%)
  local copies, waits for them, and re-layouts  0.63 us (2%)
    pallas_call x1, Pallas kernels, shards(): pl.pallas_call(functools.partial(kernel, frames), out_shape=pltpu.VMEM((R...  37.9 us

profile of v4, /device:TPU:30, one launch (start us, length us, event | category | flops | bytes accessed | tf_op | source)
XLA Modules:
  0.0 38.6 jit_solution(5811152791602747855)
XLA Ops:
  0.0 37.9 %shard_map.109 = f32[32,512]{1,0:T(8,128)S(1)} custom-call(bf16[8,256,512]{2,1,0:T(8,128)(2,1)} %bitcast.12, bf16[8,256,512]{2,1,0:T(8,128)(2,1)} %sens_hbm.1, s32[8,256]{1,0:T(8,128)} %bitcast.17, f32[32,512]{1,0:T(8,128)} %bitcast.14, bf16[2,512,512]{2,1,0:T(8,128)(2,1)} %constant.4.clone.table_hbm, bf16[6,144,64]{2,1,0:T(8,128)(2,1)} %constant.5.clone.pick_hbm, ...), custom_call_target="tpu_custom_call" | custom-call | tf_op jit(solution)/shard_map/pallas_call | solution.py:426
  37.9 0.6 %copy.13 = f32[1,32,512]{2,1,0:T(8,128)} copy(f32[1,32,512]{2,1,0:T(8,128)S(1)} %bitcast.11) | data formatting | bytes 131072

commit v5 on v4

--- a/solution.py
+++ b/solution.py
@@ -128,7 +128,7 @@
     pl.semaphore_wait(barrier, GRP - 1 + present)
 
     acopy = []
-    for s in range(1, GRP):
+    for s in (4, 1, 7, 3, 5, 2, 6):
         c = pltpu.make_async_remote_copy(
             src_ref=xb.at[pl.ds(r0, RB)],
             dst_ref=xb.at[pl.ds(r0, RB)],
@@ -143,33 +143,35 @@
     loads[7].wait()
     loads[8].wait()
 
-    def columns(q):
-        rq = pl.multiple_of(q * RB, RB)
-        xv = xb[pl.ds(rq, RB), :].astype(F32)
-        x_re, x_im = xv[:, :N], xv[:, N:]
-        for c in range(NCO):
-            sv = sens[c, pl.ds(rq, RB), :].astype(F32)
-            s_re, s_im = sv[:, :N], sv[:, N:]
-            ci[c * RB : (c + 1) * RB, :N] = (s_re * x_re - s_im * x_im).astype(BF16)
-            ci[c * RB : (c + 1) * RB, N:] = (s_re * x_im + s_im * x_re).astype(BF16)
-        for half in range(2):
-            spec = dot(ci[...], table[0, :, half * N : (half + 1) * N]).astype(BF16)
+    def columns(shifts):
+        for s in shifts:
+            rq = pl.multiple_of(lax.rem(j - s + GRP, GRP) * RB, RB)
+            xv = xb[pl.ds(rq, RB), :].astype(F32)
+            x_re, x_im = xv[:, :N], xv[:, N:]
             for c in range(NCO):
-                cols[c, pl.ds(half * ROWS + rq, RB), :] = spec[c * RB : (c + 1) * RB]
-
-    columns(j)
-
-    @pl.loop(1, GRP)
-    def _(s):
-        pltpu.make_async_remote_copy(
-            src_ref=xb.at[pl.ds(r0, RB)],
-            dst_ref=xb.at[pl.ds(pl.multiple_of(lax.rem(j - s + GRP, GRP) * RB, RB), RB)],
-            send_sem=asend.at[s],
-            recv_sem=arecv.at[s],
-            device_id={"coil": lax.rem(j + s, GRP)},
-            device_id_type=MESH,
-        ).wait_recv()
-        columns(lax.rem(j - s + GRP, GRP))
+                sv = sens[c, pl.ds(rq, RB), :].astype(F32)
+                s_re, s_im = sv[:, :N], sv[:, N:]
+                ci[s, c * RB : (c + 1) * RB, :N] = (s_re * x_re - s_im * x_im).astype(BF16)
+                ci[s, c * RB : (c + 1) * RB, N:] = (s_re * x_im + s_im * x_re).astype(BF16)
+        for s in shifts:
+            rq = pl.multiple_of(lax.rem(j - s + GRP, GRP) * RB, RB)
+            for half in range(2):
+                spec = dot(ci[s], table[0, :, half * N : (half + 1) * N]).astype(BF16)
+                for c in range(NCO):
+                    cols[c, pl.ds(half * ROWS + rq, RB), :] = spec[c * RB : (c + 1) * RB]
+
+    columns((0,))
+    for shifts in ((4, 1, 7), (3, 5), (2, 6)):
+        for s in shifts:
+            pltpu.make_async_remote_copy(
+                src_ref=xb.at[pl.ds(r0, RB)],
+                dst_ref=xb.at[pl.ds(pl.multiple_of(lax.rem(j - s + GRP, GRP) * RB, RB), RB)],
+                send_sem=asend.at[s],
+                recv_sem=arecv.at[s],
+                device_id={"coil": lax.rem(j + s, GRP)},
+                device_id_type=MESH,
+            ).wait_recv()
+        columns(shifts)
 
     loads[9].wait()
     loads[10].wait()
@@ -184,36 +186,55 @@
             stacked[c, half * ROWS : (half + 1) * ROWS, :] = dot(
                 misfit[c], table[1, :, half * N : (half + 1) * N]
             ).astype(BF16)
-    for c in range(NCO):
-        m = mask[c : c + 1, :].astype(F32).astype(BF16)
-        mm = jnp.concatenate([m, m], axis=1)
-        b_re = dot(table[0, :ROWS, :] * mm, stacked[c])
-        b_im = dot(table[0, ROWS:, :] * mm, stacked[c])
-        s_re, s_im = sens[c, :, :N].astype(F32), sens[c, :, N:].astype(F32)
-        g_re = s_re * b_re + s_im * b_im
-        g_im = s_re * b_im - s_im * b_re
-        acc[:, :N] = g_re if c == 0 else acc[:, :N] + g_re
-        acc[:, N:] = g_im if c == 0 else acc[:, N:] + g_im
-
-    xr[:ROWS, :] = pltpu.roll(acc[...], 3, axis=0)
-    xr[ROWS:, :] = pltpu.roll(acc[ROWS - 16 :, :], 3, axis=0)
-    for q in range(GRP):
-        rows = slice(q * RB, q * RB + HR)
-        gs[q] = jnp.concatenate([xr[rows, :N], xr[rows, N:]], axis=0).astype(BF16)
+    def gradient(base):
+        base = pl.multiple_of(base, 128)
+        rows = pl.ds(base, 128)
+        into = pl.ds(base + 8, 128)
+        for c in range(NCO):
+            m = mask[c : c + 1, :].astype(F32).astype(BF16)
+            mm = jnp.concatenate([m, m], axis=1)
+            b_re = dot(table[0, rows, :] * mm, stacked[c])
+            b_im = dot(table[0, pl.ds(base + ROWS, 128), :] * mm, stacked[c])
+            s_re, s_im = sens[c, rows, :N].astype(F32), sens[c, rows, N:].astype(F32)
+            g_re = s_re * b_re + s_im * b_im
+            g_im = s_re * b_im - s_im * b_re
+            acc[into, :N] = g_re if c == 0 else acc[into, :N] + g_re
+            acc[into, N:] = g_im if c == 0 else acc[into, N:] + g_im
+
+    def haloed(q):
+        v = acc[pl.ds(pl.multiple_of(q * RB, RB), HR + 8), :][5 : 5 + HR]
+        return jnp.concatenate([v[:, :N], v[:, N:]], axis=0)
 
     bcopy = []
-    for s in range(1, GRP):
-        to = lax.rem(j + s, GRP)
-        c = pltpu.make_async_remote_copy(
-            src_ref=gs.at[to],
-            dst_ref=grecv.at[s],
-            send_sem=bsend.at[s],
-            recv_sem=brecv.at[s],
-            device_id={"coil": to},
-            device_id_type=MESH,
-        )
-        c.start()
-        bcopy.append(c)
+
+    def send(targets):
+        begun = []
+        for to in targets:
+            slot = len(bcopy) + len(begun)
+            gs[slot] = haloed(to).astype(BF16)
+            s = lax.rem(to - j + GRP, GRP)
+            begun.append(
+                pltpu.make_async_remote_copy(
+                    src_ref=gs.at[slot],
+                    dst_ref=grecv.at[s],
+                    send_sem=bsend.at[s],
+                    recv_sem=brecv.at[s],
+                    device_id={"coil": to},
+                    device_id_type=MESH,
+                )
+            )
+        for c in begun:
+            c.start()
+        bcopy.extend(begun)
+
+    low = j < GRP // 2
+    acc[:8, :] = jnp.zeros((8, 2 * N), F32)
+    acc[ROWS + 8 :, :] = jnp.zeros((8, 2 * N), F32)
+    gradient(jnp.where(low, 128, 0))
+    send([jnp.where(low, 5, 0) + n for n in range(3)])
+    gradient(jnp.where(low, 0, 128))
+    start = jnp.where(low, 0, 3)
+    send([start + lax.rem(j - start + n, 5) for n in range(1, 5)])
 
     xr[:ROWS, :] = pltpu.roll(xb[...].astype(F32), 3, axis=0)
     xr[ROWS:, :] = jnp.zeros((16, 2 * N), F32)
@@ -221,7 +242,7 @@
         cut = slice(half * N, (half + 1) * N)
         xh[half * HR : (half + 1) * HR, :] = xr[pl.ds(r0, HR), cut]
         xh[half * HR + 3 : half * HR + 3 + RB, :] = image[:, cut]
-    total = xh[...] - gs[j].astype(F32)
+    total = xh[...] - haloed(j)
     for c in bcopy:
         c.wait_recv()
     for s in range(1, GRP):
@@ -435,11 +456,11 @@
             pltpu.VMEM((3, 3 * CH, 3 * CH), BF16),
             pltpu.VMEM((144, 640), BF16),
             pltpu.VMEM((ROWS, 2 * N), BF16),
-            pltpu.VMEM((NCO * RB, 2 * N), BF16),
+            pltpu.VMEM((GRP, NCO * RB, 2 * N), BF16),
             pltpu.VMEM((NCO, 2 * ROWS, N), BF16),
             pltpu.VMEM((NCO, ROWS, 2 * N), BF16),
             pltpu.VMEM((NCO, 2 * ROWS, N), BF16),
-            pltpu.VMEM((ROWS, 2 * N), F32),
+            pltpu.VMEM((ROWS + 16, 2 * N), F32),
             pltpu.VMEM((GRP, 2 * HR, N), BF16),
             pltpu.VMEM((GRP, 2 * HR, N), BF16),
             pltpu.VMEM((ROWS + 16, 2 * N), F32),

time: 39.1 us -> 37.8 us (0.967)
  Pallas kernels: 37.9 us -> 36.7 us
    pallas_call x1, Pallas kernels: 37.9 us -> 36.7 us  [shards(): pl.pallas_call(functools.partial(kernel, frames), out_shape=pltpu.VMEM((R...]
where the time goes in v5:
time: 37.8 us; the launch traced here: 37.3 us
  Pallas kernels  36.7 us (97%)
  local copies, waits for them, and re-layouts  0.63 us (2%)
    pallas_call x1, Pallas kernels, shards(): pl.pallas_call(functools.partial(kernel, frames), out_shape=pltpu.VMEM((R...  36.7 us

profile of v5, /device:TPU:30, one launch (start us, length us, event | category | flops | bytes accessed | tf_op | source)
XLA Modules:
  0.0 37.3 jit_solution(7358098510835216305)
XLA Ops:
  0.0 36.7 %shard_map.109 = f32[32,512]{1,0:T(8,128)S(1)} custom-call(bf16[8,256,512]{2,1,0:T(8,128)(2,1)} %bitcast.12, bf16[8,256,512]{2,1,0:T(8,128)(2,1)} %sens_hbm.1, s32[8,256]{1,0:T(8,128)} %bitcast.17, f32[32,512]{1,0:T(8,128)} %bitcast.14, bf16[2,512,512]{2,1,0:T(8,128)(2,1)} %constant.4.clone.table_hbm, bf16[6,144,64]{2,1,0:T(8,128)(2,1)} %constant.5.clone.pick_hbm, ...), custom_call_target="tpu_custom_call" | custom-call | tf_op jit(solution)/shard_map/pallas_call | solution.py:447
  36.7 0.6 %copy.13 = f32[1,32,512]{2,1,0:T(8,128)} copy(f32[1,32,512]{2,1,0:T(8,128)S(1)} %bitcast.11) | data formatting | bytes 131072

commit v6 on v5

--- a/solution.py
+++ b/solution.py
@@ -48,7 +48,7 @@
     return lax.broadcasted_iota(jnp.int32, shape, 0), lax.broadcasted_iota(jnp.int32, shape, 1)
 
 
-def conv_weights(pick, wf, wm, wl, bf, bm, w54, w1, w2, w3):
+def first_weights(pick, wf, w54, w1):
     w54[...] = jnp.zeros((64, CH), F32)
     for k in range(27):
         w54[2 * k : 2 * k + 2, :] = wf[k].astype(F32)
@@ -63,6 +63,9 @@
         part = lax.dot_general(tile, z, (((1,), (1,)), ((), ())), preferred_element_type=F32)
         total = jnp.where((col & 7) == base + b, part, total)
     w1[...] = total.astype(BF16)
+
+
+def other_weights(pick, wm, wl, bf, bm, w54, w2, w3):
     for k in range(27):
         w54[2 * k : 2 * k + 2, :] = wl[k].astype(F32)
     source = w54[...].astype(BF16)
@@ -123,7 +126,7 @@
     xb[pl.ds(r0, RB), :] = image[...].astype(BF16)
     for c in loads[1:7]:
         c.wait()
-    bias1, bias2 = conv_weights(pick, wf, wm, wl, bf, bm, w54, w1, w2, w3)
+    first_weights(pick, wf, w54, w1)
     present = sum(here.astype(jnp.int32) for _, here in partners)
     pl.semaphore_wait(barrier, GRP - 1 + present)
 
@@ -223,8 +226,9 @@
                     device_id_type=MESH,
                 )
             )
-        for c in begun:
-            c.start()
+            if len(begun) > 1:
+                begun[-2].start()
+        begun[-1].start()
         bcopy.extend(begun)
 
     low = j < GRP // 2
@@ -243,9 +247,16 @@
         xh[half * HR : (half + 1) * HR, :] = xr[pl.ds(r0, HR), cut]
         xh[half * HR + 3 : half * HR + 3 + RB, :] = image[:, cut]
     total = xh[...] - haloed(j)
-    for c in bcopy:
-        c.wait_recv()
-    for s in range(1, GRP):
+    bias1, bias2 = other_weights(pick, wm, wl, bf, bm, w54, w2, w3)
+    for s in (4, 3, 5, 2, 6, 1, 7):
+        pltpu.make_async_remote_copy(
+            src_ref=gs.at[0],
+            dst_ref=grecv.at[s],
+            send_sem=bsend.at[s],
+            recv_sem=brecv.at[s],
+            device_id={"coil": lax.rem(j + s, GRP)},
+            device_id_type=MESH,
+        ).wait_recv()
         total = total - grecv[s].astype(F32)
     line = lax.broadcasted_iota(jnp.int32, (2 * HR, N), 0)
     row = r0 - 3 + jnp.where(line >= HR, line - HR, line)

time: 37.8 us -> 37.9 us (level)
  no operation moved by 1% of the time
where the time goes in v6:
time: 37.9 us; the launch traced here: 37.4 us
  Pallas kernels  36.8 us (97%)
  local copies, waits for them, and re-layouts  0.63 us (2%)
    pallas_call x1, Pallas kernels, shards(): pl.pallas_call(functools.partial(kernel, frames), out_shape=pltpu.VMEM((R...  36.8 us

profile of v6, /device:TPU:30, one launch (start us, length us, event | category | flops | bytes accessed | tf_op | source)
XLA Modules:
  0.0 37.4 jit_solution(10714393650824106922)
XLA Ops:
  0.0 36.8 %shard_map.109 = f32[32,512]{1,0:T(8,128)S(1)} custom-call(bf16[8,256,512]{2,1,0:T(8,128)(2,1)} %bitcast.12, bf16[8,256,512]{2,1,0:T(8,128)(2,1)} %sens_hbm.1, s32[8,256]{1,0:T(8,128)} %bitcast.17, f32[32,512]{1,0:T(8,128)} %bitcast.14, bf16[2,512,512]{2,1,0:T(8,128)(2,1)} %constant.4.clone.table_hbm, bf16[6,144,64]{2,1,0:T(8,128)(2,1)} %constant.5.clone.pick_hbm, ...), custom_call_target="tpu_custom_call" | custom-call | tf_op jit(solution)/shard_map/pallas_call | solution.py:458
  36.8 0.6 %copy.13 = f32[1,32,512]{2,1,0:T(8,128)} copy(f32[1,32,512]{2,1,0:T(8,128)S(1)} %bitcast.11) | data formatting | bytes 131072

commit v7 on v6

--- a/solution.py
+++ b/solution.py
@@ -112,7 +112,7 @@
     for c in loads:
         c.start()
 
-    partners = [(d, (t + d >= 0) & (t + d < frames)) for d in (-2, 2, -1, 1)]
+    partners = [(d, (t + d >= 0) & (t + d < frames)) for d in (-1, 1, -2, 2)]
 
     barrier = pltpu.get_barrier_semaphore()
     for s in range(1, GRP):

time: 37.9 us -> 37.5 us (0.989)
  the two profiles are of different devices: /device:TPU:30 before, /device:TPU:22 now
where the time goes in v7:
time: 37.5 us; the launch traced here: 37.4 us
  Pallas kernels  36.8 us (98%)
  local copies, waits for them, and re-layouts  0.63 us (2%)
    pallas_call x1, Pallas kernels, shards(): pl.pallas_call(functools.partial(kernel, frames), out_shape=pltpu.VMEM((R...  36.8 us

profile of v7, /device:TPU:22, one launch (start us, length us, event | category | flops | bytes accessed | tf_op | source)
XLA Modules:
  0.0 37.4 jit_solution(9579141919620122595)
XLA Ops:
  0.0 36.8 %shard_map.109 = f32[32,512]{1,0:T(8,128)S(1)} custom-call(bf16[8,256,512]{2,1,0:T(8,128)(2,1)} %bitcast.12, bf16[8,256,512]{2,1,0:T(8,128)(2,1)} %sens_hbm.1, s32[8,256]{1,0:T(8,128)} %bitcast.17, f32[32,512]{1,0:T(8,128)} %bitcast.14, bf16[2,512,512]{2,1,0:T(8,128)(2,1)} %constant.4.clone.table_hbm, bf16[6,144,64]{2,1,0:T(8,128)(2,1)} %constant.5.clone.pick_hbm, ...), custom_call_target="tpu_custom_call" | custom-call | tf_op jit(solution)/shard_map/pallas_call | solution.py:458
  36.8 0.6 %copy.13 = f32[1,32,512]{2,1,0:T(8,128)} copy(f32[1,32,512]{2,1,0:T(8,128)S(1)} %bitcast.11) | data formatting | bytes 131072
